TPU v7x, 128 devices: a whole 4x4x4 slice. The times are simulated.
128 devices in a mesh: section: 2 (over y_hi), dp: 64 (over z, x, y_lo, core).
Axes of the slice: x: 4, y: 4 (y_hi: 2, y_lo: 2; y = y_hi * 2 + y_lo), z: 4, core: 2. Of those that a mesh axis runs over, the one named last changes fastest.
Arguments:
- layer_inputs: bfloat16 [2, 16384, 4096], P('section', 'dp'), may hold values from -20 to 20
- norm_gain: float32 [2, 4096], P('section'), may hold values from 0.5 to 1.5
- queries: bfloat16 [2, 16384, 2048], P('section', 'dp'), may hold values from -100 to 100
- output_gradient: bfloat16 [2, 16384, 2048], P('section', 'dp'), may hold values from -6 to 6
- w_key: bfloat16 [2, 4096, 512], P('section'), may hold values from -0.09375 to 0.09375
- value_matrix: bfloat16 [2, 4096, 512], P('section'), may hold values from -0.09375 to 0.09375
- top_grad: bfloat16 [16384, 4096], P('dp'), may hold values from -6 to 6
Outputs:
- key_grad: bfloat16 [2, 4096, 512], P('section')
- value_grad: bfloat16 [2, 4096, 512], P('section')
- input_grad: bfloat16 [2, 16384, 4096], P('section', 'dp')
All inputs are finite; a program needn't handle non-finite values.
Results may differ from a plain program's by a relative error of at most 0.0082.
Values may be sent and summed in bfloat16 or wider, within the bound.
No kernel may reach another device: no remote copies, remote signals or barrier semaphores. Data moves between devices by JAX's collectives and lax.ppermute only.
A program may use at most 128 MiB of HBM per device.

v0:
```python
import jax
import jax.numpy as jnp
from jax import lax
from jax.sharding import PartitionSpec as P

HEAD_SIZE = 128
KEY_VALUE_HEADS = 4
SEQUENCE_TOKENS = 128


epsilon = 1e-05


def shifted(value, axis, steps):
    count = lax.axis_size(axis)
    initial, last = (max(0, -steps), min(count, count - steps))
    return lax.ppermute(value, axis, [(source, source + steps) for source in range(initial, last)])


def normalize(block_inputs, gain_row):
    wide_inputs = block_inputs.astype(jnp.float32)
    inv_rms = lax.rsqrt(jnp.mean(wide_inputs * wide_inputs, axis=-1, keepdims=True) + epsilon)
    return (wide_inputs, inv_rms, (wide_inputs * inv_rms * gain_row).astype(jnp.bfloat16))


def value_pass(heads_of_query, heads_of_key, head_gradients):
    scale = HEAD_SIZE ** (-0.5)
    scores = (
        jnp.einsum(
            "btjgd,bsjd->bjgts", heads_of_query, heads_of_key, preferred_element_type=jnp.float32
        )
        * scale
    )
    causal = lax.broadcasted_iota(
        jnp.int32, (SEQUENCE_TOKENS, SEQUENCE_TOKENS), 0
    ) >= lax.broadcasted_iota(jnp.int32, (SEQUENCE_TOKENS, SEQUENCE_TOKENS), 1)
    scores = jnp.where(causal, scores, -1e30)
    row_max = jnp.max(scores, axis=-1, keepdims=True)
    weight = jnp.exp(scores - row_max)
    probability = weight / jnp.sum(weight, axis=-1, keepdims=True)
    value_gradient = jnp.einsum(
        "bjgts,btjgd->bsjd",
        probability.astype(jnp.bfloat16),
        head_gradients,
        preferred_element_type=jnp.float32,
    )
    return (probability, value_gradient.astype(jnp.bfloat16))


def key_pass(probability, heads_of_query, heads_of_value, head_gradients):
    scale = HEAD_SIZE ** (-0.5)
    grad_prob = jnp.einsum(
        "btjgd,bsjd->bjgts", head_gradients, heads_of_value, preferred_element_type=jnp.float32
    )
    row_delta = jnp.sum(probability * grad_prob, axis=-1, keepdims=True)
    dscore = (probability * (grad_prob - row_delta) * scale).astype(jnp.bfloat16)
    key_gradient = jnp.einsum(
        "bjgts,btjgd->bsjd", dscore, heads_of_query, preferred_element_type=jnp.float32
    )
    return key_gradient.astype(jnp.bfloat16)


def weight_term(normed, grad_proj):
    return jnp.einsum("td,tk->dk", normed, grad_proj, preferred_element_type=jnp.float32)


def input_term(
    wide_inputs, inv_rms, gain_row, key_gradient, value_gradient, key_weight, value_weight
):
    grad_norm = jnp.einsum(
        "tk,dk->td", key_gradient, key_weight, preferred_element_type=jnp.float32
    )
    grad_norm = grad_norm + jnp.einsum(
        "tk,dk->td", value_gradient, value_weight, preferred_element_type=jnp.float32
    )
    scaled = gain_row * grad_norm
    return inv_rms * scaled - wide_inputs * inv_rms**3 * jnp.mean(
        wide_inputs * scaled, axis=-1, keepdims=True
    )


def layer_grads(
    block_inputs,
    gain_row,
    block_query_rows,
    block_output_gradient,
    key_weight,
    value_weight,
    value_hook,
):
    wide_inputs, inv_rms, normed = normalize(block_inputs, gain_row)
    key_projected = jnp.dot(normed, key_weight, preferred_element_type=jnp.float32).astype(
        jnp.bfloat16
    )
    value_projected = jnp.dot(normed, value_weight, preferred_element_type=jnp.float32).astype(
        jnp.bfloat16
    )
    count_of_rows = block_inputs.shape[0]
    sequence_count = count_of_rows // SEQUENCE_TOKENS
    heads_of_query = block_query_rows.reshape(
        sequence_count, SEQUENCE_TOKENS, KEY_VALUE_HEADS, -1, HEAD_SIZE
    )
    head_gradients = block_output_gradient.reshape(
        sequence_count, SEQUENCE_TOKENS, KEY_VALUE_HEADS, -1, HEAD_SIZE
    )
    heads_of_key = key_projected.reshape(
        sequence_count, SEQUENCE_TOKENS, KEY_VALUE_HEADS, HEAD_SIZE
    )
    heads_of_value = value_projected.reshape(
        sequence_count, SEQUENCE_TOKENS, KEY_VALUE_HEADS, HEAD_SIZE
    )
    probability, value_gradient = value_pass(heads_of_query, heads_of_key, head_gradients)
    value_gradient = value_gradient.reshape(count_of_rows, KEY_VALUE_HEADS * HEAD_SIZE)
    value_partial = value_hook(weight_term(normed, value_gradient))
    key_gradient = key_pass(probability, heads_of_query, heads_of_value, head_gradients).reshape(
        count_of_rows, KEY_VALUE_HEADS * HEAD_SIZE
    )
    key_partial = weight_term(normed, key_gradient)
    layer_dx = input_term(
        wide_inputs, inv_rms, gain_row, key_gradient, value_gradient, key_weight, value_weight
    )
    return (key_partial, value_partial, layer_dx)


def sum_values(partial_value):
    return lax.psum(partial_value, "dp")


def per_device(layer_inputs, norm_gain, queries, output_gradient, w_key, value_matrix, top_grad):
    layer_count = layer_inputs.shape[0]
    count_of_rows = layer_inputs.shape[1]
    replicas = lax.axis_size("dp")
    is_last = lax.axis_index("section") == lax.axis_size("section") - 1
    residual = jnp.zeros((count_of_rows, layer_inputs.shape[2]), jnp.float32)
    key_sums = [None] * layer_count
    value_sums = [None] * layer_count
    for layer_index in reversed(range(layer_count)):
        key_partial, value_partial, layer_dx = layer_grads(
            layer_inputs[layer_index],
            norm_gain[layer_index],
            queries[layer_index],
            output_gradient[layer_index],
            w_key[layer_index],
            value_matrix[layer_index],
            sum_values,
        )
        key_sums[layer_index] = lax.psum(key_partial, "dp")
        value_sums[layer_index] = value_partial
        residual = layer_dx
    key_stack = jnp.stack(key_sums)
    value_stack = jnp.stack(value_sums)
    key_grad = (key_stack / replicas).astype(jnp.bfloat16)
    value_grad = (value_stack / replicas).astype(jnp.bfloat16)
    own_total = residual + jnp.where(is_last, top_grad.astype(jnp.float32), 0.0)
    outgoing = own_total.astype(jnp.bfloat16)
    received = shifted(outgoing, "section", -1)
    input_grad = (received.astype(jnp.float32) + own_total).astype(jnp.bfloat16)
    return (key_grad, value_grad, input_grad[None])


def solution(mesh):
    in_specs = (
        P("section", "dp", None),
        P("section", None),
        P("section", "dp", None),
        P("section", "dp", None),
        P("section", None, None),
        P("section", None, None),
        P("dp", None),
    )
    out_specs = (P("section", None, None), P("section", None, None), P("section", "dp", None))
    return jax.shard_map(
        per_device, mesh=mesh, in_specs=in_specs, out_specs=out_specs, check_vma=False
    )
```

profile of v0, /device:TPU:16, one launch (start us, length us, event | category | flops | bytes accessed | tf_op | source)
XLA Modules:
  0.0 683.1 jit_solution(12803363551988181715)
XLA Ops:
  7.2 0.0 copy-start
  7.2 0.0 copy-start.3
  7.2 0.0 all-reduce.3.cloned.1.call-start
  7.3 1.9 reshape_squeeze.7
  9.2 2.1 fusion.6
  11.3 0.0 copy-done
  11.3 0.0 copy-done.3
  11.3 4.2 fusion.35
  15.5 1.0 reshape.102
  16.5 2.6 reshape_squeeze.6
  19.1 4.2 fusion.32
  23.2 1.7 reshape.101
  24.9 1.8 fusion.47
  26.7 3.5 fusion.85
  30.2 2.0 fusion.38
  32.3 4.6 fusion.39
  36.9 0.2 copy.21
  37.1 4.6 fusion.56
  41.8 0.2 copy.23
  42.0 4.6 fusion.53
  46.6 0.0 all-reduce.3.cloned.1.call-update
  46.6 0.0 copy-start.2
  46.6 3.6 fusion.18
  50.2 0.0 copy-done.2
  50.3 0.0 copy-start.1
  50.3 1.6 fusion.10
  51.9 1.5 fusion.80
  53.5 2.5 collective-permute-start
  56.0 88.2 %collective-permute-done = bf16[256,4096]{1,0:T(8,128)(2,1)S(1)} collective-permute-done((bf16[256,4096]{1,0:T(8,128)(2,1)S(1)}, bf16[256,4096]{1,0:T(8,128)(2,1)S(1)}, u32[]{:S(2)}, u32[]{:S(2)}) %collective-permute-start) | collective-permute-done | bytes 2097184 | tf_op jit(solution)/shard_map/ppermute | solution.py:17
  144.2 3.2 fusion.22
  147.4 517.3 %all-reduce.3.cloned.1.call-done = (f32[4096,512]{1,0:T(8,128)}, f32[4096,512]{1,0:T(8,128)}) async-done(((f32[4096,512]{1,0:T(8,128)}, f32[4096,512]{1,0:T(8,128)}), (f32[4096,512]{1,0:T(8,128)}, f32[4096,512]{1,0:T(8,128)})) %all-reduce.3.cloned.1.call-update) | async-done | bytes 16777232 | tf_op jit(solution)/shard_map/psum | solution.py:147
  664.7 11.6 %fusion.13 = (bf16[1,4096,512]{2,1,0:T(8,128)(2,1)}, bf16[1,4096,512]{2,1,0:T(8,128)(2,1)}) fusion(f32[4096,512]{1,0:T(8,128)} %get-tuple-element.3, f32[4096,512]{1,0:T(8,128)} %get-tuple-element.4), kind=kLoop, calls=%fused_computation.18 | loop fusion | flops 8388608 | bytes 25165824 | tf_op jit(solution)/shard_map/convert_element_type | solution.py:152
  (4 shorter events, 0.0 us)
Async XLA Ops:
  7.2 4.1 copy-start
  7.2 4.1 copy-start.3
  7.2 657.5 %all-reduce.3.cloned.1.call-start = ((), (), s32[]{:S(2)}) async-start(), calls=%async_computation | async-start | bytes 33554432 | tf_op jit(solution)/shard_map/psum | solution.py:147
  46.6 3.6 copy-start.2
  50.3 1.7 copy-start.1
  53.5 90.7 %collective-permute-start = (bf16[256,4096]{1,0:T(8,128)(2,1)S(1)}, bf16[256,4096]{1,0:T(8,128)(2,1)S(1)}, u32[]{:S(2)}, u32[]{:S(2)}) collective-permute-start(bf16[256,4096]{1,0:T(8,128)(2,1)S(1)} %fusion.80), channel_id=1, source_target_pairs={{64,0},{65,1},{66,2},{67,3},{68,4},{69,5},{70,6},{71,7},{72,8},{73... | collective-permute-start | bytes 6291464 | tf_op jit(solution)/shard_map/ppermute | solution.py:17
Sparse Core Ops, SparseCore 0:
  46.7 617.9 all-reduce.2
where the time goes:
time: 684 us; the launch traced here: 683 us
  waiting for transfers between devices  606 us (89%)
  matrix products  34.8 us (5%)
  other arithmetic  18.4 us (3%)
  between operations  14.2 us (2%)
  local copies, waits for them, and re-layouts  7.65 us (1%)
    psum x1, waiting for transfers between devices, per_device(): key_sums[layer_index] = lax.psum(key_partial, 'dp')  517 us
    ppermute x1, waiting for transfers between devices, shifted(): lax.ppermute(value, axis, [(source, source + steps) for source in range(i...  88.2 us
  transfers between devices with their start and end apart: 2, of which 2 were waited for; matrix products, arithmetic and copies ran while one was open for 1% of the time, Pallas kernels for 0%

commit v1 on v0

v1 whole, which is shorter than its diff:
```python
import jax
import jax.numpy as jnp
from jax import lax
from jax.experimental import pallas as pl
from jax.experimental.pallas import tpu as pltpu
from jax.sharding import Mesh
from jax.sharding import PartitionSpec as P

HEAD = 128
WIDTH = 4096
COLS = 512
ROWS = 256
REPLICAS = 64
epsilon = 1e-05
SCALE = HEAD ** (-0.5)


bf16 = jnp.bfloat16
f32 = jnp.float32


def shape(dims, dtype):
    return jax.ShapeDtypeStruct(dims, dtype)


def vmem():
    return pl.BlockSpec(memory_space=pltpu.VMEM)


def held(dims, dtype):
    return pltpu.VMEM(dims, dtype)


def hold(*arrays):
    return tuple(pltpu.with_memory_space_constraint(a, pltpu.VMEM) for a in arrays)


def smem():
    return pl.BlockSpec(memory_space=pltpu.SMEM)


def budget(mebibytes):
    return pltpu.CompilerParams(vmem_limit_bytes=mebibytes << 20)


def project_body(place, x, gain, wk, wv, send, mine, keys, values, inverse, acc_k, acc_v, inv):
    step = pl.program_id(0)
    tile = (step + 4 * (1 - place[3])) % 8

    @pl.when(step == 0)
    def _():
        total = jnp.zeros((ROWS, 128), f32)
        for i in range(WIDTH // 128):
            part = x[:, i * 128 : (i + 1) * 128].astype(f32)
            total = total + part * part
        mean = jnp.sum(total, axis=1, keepdims=True) / WIDTH
        inv[...] = jnp.broadcast_to(lax.rsqrt(mean + epsilon), (ROWS, 128))
        inverse[...] = inv[...]
        acc_k[...] = jnp.zeros_like(acc_k)
        acc_v[...] = jnp.zeros_like(acc_v)

    part = x[:, pl.ds(pl.multiple_of(tile * 512, 512), 512)].astype(f32)
    normed = (part * inv[:, :1] * gain[...]).astype(bf16)

    @pl.when(step < 4)
    def _():
        send[...] = normed

    @pl.when(step >= 4)
    def _():
        mine[...] = normed

    acc_k[...] += jnp.dot(normed, wk[...], preferred_element_type=f32)
    acc_v[...] += jnp.dot(normed, wv[...], preferred_element_type=f32)

    @pl.when(step == 7)
    def _():
        keys[...] = acc_k[...]
        values[...] = acc_v[...]


def project(place, x, gain, wk, wv):
    tile = lambda i, p: (i + 4 * (1 - p[3])) % 8
    return pl.pallas_call(
        project_body,
        grid_spec=pltpu.PrefetchScalarGridSpec(
            num_scalar_prefetch=1,
            grid=(8,),
            in_specs=[
                pl.BlockSpec((ROWS, WIDTH), lambda i, p: (0, 0)),
                pl.BlockSpec((1, 512), lambda i, p: (0, tile(i, p))),
                pl.BlockSpec((512, COLS), lambda i, p: (tile(i, p), 0)),
                pl.BlockSpec((512, COLS), lambda i, p: (tile(i, p), 0)),
            ],
            out_specs=[
                pl.BlockSpec((ROWS, 512), lambda i, p: (0, jnp.minimum(i, 3))),
                pl.BlockSpec((ROWS, 512), lambda i, p: (0, jnp.maximum(i - 4, 0))),
                pl.BlockSpec((ROWS, COLS), lambda i, p: (0, 0)),
                pl.BlockSpec((ROWS, COLS), lambda i, p: (0, 0)),
                pl.BlockSpec((ROWS, 128), lambda i, p: (0, 0)),
            ],
            scratch_shapes=[
                pltpu.VMEM((ROWS, COLS), f32),
                pltpu.VMEM((ROWS, COLS), f32),
                pltpu.VMEM((ROWS, 128), f32),
            ],
        ),
        out_shape=[
            shape((ROWS, 2048), bf16),
            shape((ROWS, 2048), bf16),
            shape((ROWS, COLS), f32),
            shape((ROWS, COLS), f32),
            shape((ROWS, 128), f32),
        ],
        cost_estimate=pl.CostEstimate(flops=2 * ROWS * WIDTH * 1024, bytes_accessed=12 << 20, transcendentals=0),
        name="project",
        compiler_params=budget(24),
    )(place, x, gain, wk, wv)


def attend_body(q, og, kf, vf, gk, gv, row):
    def heads(ref):
        return jnp.concatenate([ref[:, h * HEAD : (h + 1) * HEAD] for h in range(4)], axis=0)

    nt = (((1,), (1,)), ((), ()))
    q4 = heads(q)
    g4 = heads(og)
    key = kf[...]
    value = vf[...]
    scores = lax.dot_general(key.astype(bf16), q4, nt, preferred_element_type=f32) * SCALE
    key_at = lax.broadcasted_iota(jnp.int32, (HEAD, 512), 0)
    query_at = lax.broadcasted_iota(jnp.int32, (HEAD, 512), 1) & (HEAD - 1)
    scores = jnp.where(key_at <= query_at, scores, -1e30)
    weight = jnp.exp(scores - jnp.max(scores, axis=0, keepdims=True))
    prob = weight / jnp.sum(weight, axis=0, keepdims=True)
    grad_value = jnp.dot(prob.astype(bf16), g4, preferred_element_type=f32).astype(bf16)
    grad_prob = lax.dot_general(value.astype(bf16), g4, nt, preferred_element_type=f32)
    delta = jnp.sum(prob * grad_prob, axis=0, keepdims=True)
    dscore = (prob * (grad_prob - delta) * SCALE).astype(bf16)
    grad_key = jnp.dot(dscore, q4, preferred_element_type=f32).astype(bf16)
    gk[...] = grad_key
    gv[...] = grad_value
    term = grad_key.astype(f32) * key + grad_value.astype(f32) * value

    @pl.when(pl.program_id(1) == 0)
    def _():
        row[...] = term

    @pl.when(pl.program_id(1) != 0)
    def _():
        row[...] += term


def attend(q, og, kf, vf):
    wide = pl.BlockSpec((128, 512), lambda s, j: (s, j))
    head = pl.BlockSpec((128, 128), lambda s, j: (s, j))
    return pl.pallas_call(
        attend_body,
        grid=(2, 4),
        in_specs=[wide, wide, head, head],
        out_specs=[head, head, pl.BlockSpec((128, 128), lambda s, j: (s, 0))],
        out_shape=[shape((ROWS, COLS), bf16), shape((ROWS, COLS), bf16), shape((ROWS, 128), f32)],
        cost_estimate=pl.CostEstimate(flops=600_000_000 * 4, bytes_accessed=4 << 20, transcendentals=1 << 19),
        name="attend",
        compiler_params=budget(16),
    )(q, og, kf, vf)


def weight_body(place, mine, theirs, grad, grad_theirs, own, *sends, axis):
    tn = (((0,), (0,)), ((), ()))
    for k in (1, 3, 2, 0):
        start = pl.multiple_of(((place[axis] + k) % 4) * 512, 512)
        part = lax.dot_general(
            mine[:, pl.ds(start, 512)], grad[...], tn, preferred_element_type=f32
        ) + lax.dot_general(
            theirs[:, pl.ds(start, 512)], grad_theirs[...], tn, preferred_element_type=f32
        )
        if k == 0:
            own[...] = part
        else:
            sends[k - 1][...] = part.astype(bf16)


def weight_parts(place, mine, theirs, grad, grad_theirs, axis):
    return pl.pallas_call(
        lambda *refs: weight_body(*refs, axis=axis),
        in_specs=[smem()] + [vmem()] * 4,
        out_specs=[vmem()] * 4,
        out_shape=[held((512, COLS), f32)] + [held((512, COLS), bf16)] * 3,
        cost_estimate=pl.CostEstimate(flops=2 * 512 * 2048 * 512, bytes_accessed=5 << 20, transcendentals=0),
        name="weight_parts",
        compiler_params=budget(8),
    )(place, *hold(mine, theirs, grad, grad_theirs))


def input_body(place, gk, gv, wk, wv, x, top, gain, inverse, row, own, lower, upper):
    nt = (((1,), (1,)), ((), ()))
    grad_norm = lax.dot_general(gk[...], wk[...], nt, preferred_element_type=f32)
    grad_norm = grad_norm + lax.dot_general(gv[...], wv[...], nt, preferred_element_type=f32)
    inv = inverse[:, :1]
    mean = jnp.sum(row[...], axis=1, keepdims=True) * (1.0 / WIDTH)
    total = inv * (gain[...] * grad_norm) - x[...].astype(f32) * (inv * inv * mean)
    total = total + jnp.where(place[4] == 1, top[...].astype(f32), 0.0)
    own[...] = total
    low = total.astype(bf16)
    lower[...] = low[:128]
    upper[...] = low[128:]


def input_terms(place, gk, gv, wk, wv, x, top, gain, inverse, row):
    whole = lambda dims: pl.BlockSpec(dims, lambda i, p: (0, 0))
    tile = lambda rows: pl.BlockSpec((rows, 512), lambda i, p: (0, i))
    weight = pl.BlockSpec((512, COLS), lambda i, p: (i, 0))
    return pl.pallas_call(
        input_body,
        grid_spec=pltpu.PrefetchScalarGridSpec(
            num_scalar_prefetch=1,
            grid=(8,),
            in_specs=[
                whole((ROWS, COLS)),
                whole((ROWS, COLS)),
                weight,
                weight,
                tile(ROWS),
                tile(ROWS),
                tile(1),
                whole((ROWS, 128)),
                whole((ROWS, 128)),
            ],
            out_specs=[tile(ROWS), tile(128), tile(128)],
        ),
        out_shape=[shape((ROWS, WIDTH), f32), shape((128, WIDTH), bf16), shape((128, WIDTH), bf16)],
        cost_estimate=pl.CostEstimate(flops=2 * ROWS * WIDTH * 1024, bytes_accessed=18 << 20, transcendentals=0),
        name="input_terms",
        compiler_params=budget(24),
    )(place, gk, gv, wk, wv, x, top, gain, inverse, row)


def finish_body(own, lower, upper, out):
    half = pl.program_id(0)

    @pl.when(half == 0)
    def _():
        out[...] = (lower[...].astype(f32) + own[...]).astype(bf16)

    @pl.when(half == 1)
    def _():
        out[...] = (upper[...].astype(f32) + own[...]).astype(bf16)


def finish(own, lower, upper):
    return pl.pallas_call(
        finish_body,
        grid=(2, 4),
        in_specs=[
            pl.BlockSpec((128, 1024), lambda h, i: (h, i)),
            pl.BlockSpec((128, 1024), lambda h, i: (0, jnp.where(h == 0, i, 3))),
            pl.BlockSpec((128, 1024), lambda h, i: (0, jnp.where(h == 0, 0, i))),
        ],
        out_specs=pl.BlockSpec((128, 1024), lambda h, i: (h, i)),
        out_shape=shape((ROWS, WIDTH), bf16),
        cost_estimate=pl.CostEstimate(flops=ROWS * WIDTH, bytes_accessed=8 << 20, transcendentals=0),
        name="finish",
        compiler_params=budget(8),
    )(own, lower, upper)


def sum_body(place, own, r1, r2, r3, out, *sends, axis):
    for k in (1, 3, 2, 0):
        rows = pl.ds(pl.multiple_of(((place[axis] + k) % 4) * 128, 128), 128)
        part = own[rows, :] + r1[rows, :].astype(f32) + r2[rows, :].astype(f32)
        part = part + r3[rows, :].astype(f32)
        if k == 0:
            out[...] = part
        else:
            sends[k - 1][...] = part.astype(bf16)


def sum_parts(place, own, received, axis):
    return pl.pallas_call(
        lambda *refs: sum_body(*refs, axis=axis),
        in_specs=[smem()] + [vmem()] * 4,
        out_specs=[vmem()] * 4,
        out_shape=[held((128, COLS), f32)] + [held((128, COLS), bf16)] * 3,
        name="sum_parts",
        compiler_params=budget(4),
    )(place, *hold(own, *received))


def pair_body(place, v0, v1, v2, v3, k0, k1, k2, k3, mine, send):
    for at, refs in ((0, (v0, v1, v2, v3)), (64, (k0, k1, k2, k3))):
        for own in (False, True):
            start = (place[2] if own else 1 - place[2]) * 64
            rows = pl.ds(pl.multiple_of(start, 64), 64)
            part = refs[0][rows, :]
            for ref in refs[1:]:
                part = part + ref[rows, :].astype(f32)
            if own:
                mine[at : at + 64, :] = part
            else:
                send[at : at + 64, :] = part.astype(bf16)


def pair_parts(place, value, value_received, key, key_received):
    return pl.pallas_call(
        pair_body,
        in_specs=[smem()] + [vmem()] * 8,
        out_specs=[vmem()] * 2,
        out_shape=[held((128, COLS), f32), held((128, COLS), bf16)],
        name="pair_parts",
        compiler_params=budget(4),
    )(place, *hold(value, *value_received, key, *key_received))


def join_body(place, block, other, value, key):
    for own, ref in ((True, block), (False, other)):
        rows = pl.ds(pl.multiple_of((place[2] if own else 1 - place[2]) * 64, 64), 64)
        value[rows, :] = ref[:64, :]
        key[rows, :] = ref[64:, :]


def join(place, block, other):
    return pl.pallas_call(
        join_body,
        in_specs=[smem()] + [vmem()] * 2,
        out_specs=[vmem()] * 2,
        out_shape=[held((128, COLS), bf16)] * 2,
        name="join",
        compiler_params=budget(4),
    )(place, *hold(block, other))


def stack_body(place, own, r1, r2, r3, out, *, axis):
    for k, ref in enumerate((own, r1, r2, r3)):
        rows = pl.ds(pl.multiple_of(((place[axis] - k + 4) % 4) * 128, 128), 128)
        out[rows, :] = ref[...]


def stack(place, own, received, axis):
    return pl.pallas_call(
        lambda *refs: stack_body(*refs, axis=axis),
        in_specs=[smem()] + [vmem()] * 4,
        out_specs=vmem(),
        out_shape=held((512, COLS), bf16),
        name="stack",
        compiler_params=budget(4),
    )(place, *hold(own, *received))


def assemble(place, value_pieces, key_pieces, value_swapped, key_swapped, ks, start=None):
    groups = []
    for k in ks:
        groups += [(0, k, 0, value_pieces[k]), (1, k, 0, key_pieces[k])]
        groups += [(0, k, 1, value_swapped[k]), (1, k, 1, key_swapped[k])]
    count = len(groups)
    extra = 0 if start is None else 2

    def body(*refs):
        place = refs[0]
        pieces = refs[1 : 1 + count]
        outs = refs[1 + count + extra : 3 + count + extra]
        sems = refs[3 + count + extra]
        copies = []
        for i, (which, k, swapped, _) in enumerate(groups):
            core = (1 - place[3]) if swapped else place[3]
            member = (place[which] - k + 4) % 4
            rows = pl.ds(pl.multiple_of(core * 2048 + member * 512, 512), 512)
            copies.append(pltpu.make_async_copy(pieces[i], outs[which].at[rows, :], sems.at[i]))
        for copy in copies:
            copy.start()
        for copy in copies:
            copy.wait()

    anywhere = pl.BlockSpec(memory_space=pl.ANY)
    return pl.pallas_call(
        body,
        in_specs=[smem()] + [vmem()] * count + [anywhere] * extra,
        out_specs=[anywhere] * 2,
        out_shape=[shape((WIDTH, COLS), bf16)] * 2,
        scratch_shapes=[pltpu.SemaphoreType.DMA((count,))],
        input_output_aliases={} if start is None else {1 + count: 0, 2 + count: 1},
        name="assemble",
        compiler_params=budget(4),
    )(place, *hold(*[g[3] for g in groups]), *(() if start is None else start))


def ring(value, axis, steps):
    count = lax.axis_size(axis)
    return lax.ppermute(value, axis, [(i, (i + steps) % count) for i in range(count)])


def down(value):
    return lax.ppermute(value, "s", [(1, 0)])


def exchange(value_sends, key_sends, value_axis, key_axis):
    value_got, key_got = [None] * 3, [None] * 3
    for k in (1, 3, 2):
        value_got[k - 1] = ring(value_sends[k - 1], value_axis, k)
        key_got[k - 1] = ring(key_sends[k - 1], key_axis, k)
    return value_got, key_got


X, Z = 0, 1


def all_steps(layer_inputs, norm_gain, queries, output_gradient, w_key, value_matrix, top_grad):
    place = jnp.stack([lax.axis_index(a).astype(jnp.int32) for a in ("x", "z", "y", "c", "s")])
    x, wk, wv = layer_inputs[0], w_key[0], value_matrix[0]
    send, mine, keys, values, inverse = project(place, x, norm_gain, wk, wv)
    theirs = ring(send, "c", 1)
    gk, gv, row = attend(queries[0], output_gradient[0], keys, values)
    gv_theirs = ring(gv, "c", 1)
    gk_theirs = ring(gk, "c", 1)
    value_own, *value_sends = weight_parts(place, mine, theirs, gv, gv_theirs, X)
    key_own, *key_sends = weight_parts(place, mine, theirs, gk, gk_theirs, Z)
    value_got, key_got = exchange(value_sends, key_sends, "x", "z")
    own, lower, upper = input_terms(place, gk, gv, wk, wv, x, top_grad, norm_gain, inverse, row)
    lower_got = down(lower)
    value_own, *value_sends = sum_parts(place, value_own, value_got, Z)
    key_own, *key_sends = sum_parts(place, key_own, key_got, X)
    value_got, key_got = exchange(value_sends, key_sends, "z", "x")
    pair, pair_send = pair_parts(place, value_own, value_got, key_own, key_got)
    pair = pair + ring(pair_send, "y", 1).astype(f32)
    block = (pair / REPLICAS).astype(bf16)
    block_other = ring(block, "y", 1)
    value_block, key_block = join(place, block, block_other)
    upper_got = down(upper)
    value_got, key_got = exchange([value_block] * 3, [key_block] * 3, "z", "x")
    value_piece = stack(place, value_block, value_got, Z)
    key_piece = stack(place, key_block, key_got, X)
    value_got, key_got = exchange([value_piece] * 3, [key_piece] * 3, "x", "z")
    value_pieces = [value_piece] + value_got
    key_pieces = [key_piece] + key_got
    value_swapped = [ring(p, "c", 1) for p in value_pieces]
    key_swapped = [ring(p, "c", 1) for p in key_pieces]
    part = assemble(place, value_pieces, key_pieces, value_swapped, key_swapped, (0, 1))
    value_grad, key_grad = assemble(
        place, value_pieces, key_pieces, value_swapped, key_swapped, (3, 2), part
    )
    input_grad = finish(own, lower_got, upper_got)
    return (key_grad[None], value_grad[None], input_grad[None])


def solution(mesh):
    wide = Mesh(mesh.devices.reshape(2, 4, 4, 2, 2), ("s", "z", "x", "y", "c"))
    dp = ("z", "x", "y", "c")
    in_specs = (
        P("s", dp, None),
        P("s", None),
        P("s", dp, None),
        P("s", dp, None),
        P("s", None, None),
        P("s", None, None),
        P(dp, None),
    )
    out_specs = (P("s", None, None), P("s", None, None), P("s", dp, None))
    return jax.shard_map(
        all_steps, mesh=wide, in_specs=in_specs, out_specs=out_specs, check_vma=False
    )
```

time: 684 us -> 182 us (0.27)
  waiting for transfers between devices: 606 us -> 85.9 us
  starting transfers between devices: 2.52 us -> 52.3 us
  matrix products: 34.8 us -> 0 us
  Pallas kernels: 0 us -> 34.2 us
  other arithmetic: 18.4 us -> 0.03 us
  between operations: 14.2 us -> 1.06 us
    psum x1 -> x0, waiting for transfers between devices: 517 us -> none  [per_device(): key_sums[layer_index] = lax.psum(key_partial, 'dp')]
    ppermute x1 -> x39, starting transfers between devices: 2.48 us -> 52.3 us  [the longest x37 47.5 us: ring(): lax.ppermute(value, axis, [(i, (i + steps) % count) for i in range(count)])]
    pallas_call x0 -> x14, Pallas kernels: none -> 34.2 us  [the longest x1 6.32 us: project(): pl.pallas_call(project_body, grid_spec=pltpu.PrefetchScalarGridSpec(num_s...]
    dot_general x9 -> x0, matrix products: 31.3 us -> none  [the longest x2 9.22 us: weight_term(): jnp.einsum('td,tk->dk', normed, grad_proj, preferred_element_type=jnp.flo...]
    convert_element_type x2 -> x1, other arithmetic: 13.1 us -> 0.03 us  [all_steps(): block = (pair / REPLICAS).astype(bf16)]
    ppermute x1 -> x39, waiting for transfers between devices: 88.2 us -> 85.9 us  [the longest x37 85.9 us: ring(): lax.ppermute(value, axis, [(i, (i + steps) % count) for i in range(count)])]
  transfers between devices with their start and end apart: 2 -> 39, of which waited for: 2 -> 15; matrix products, arithmetic and copies ran while one was open for 1% -> 0% of each run, Pallas kernels for 0% -> 13%
where the time goes in v1:
time: 182 us; the launch traced here: 180 us
  waiting for transfers between devices  85.9 us (47%)
  starting transfers between devices  52.3 us (29%)
  Pallas kernels  34.2 us (19%)
  local copies, waits for them, and re-layouts  6.78 us (4%)
    ppermute x37, waiting for transfers between devices, ring(): lax.ppermute(value, axis, [(i, (i + steps) % count) for i in range(count)])  85.9 us
    ppermute x37, starting transfers between devices, ring(): lax.ppermute(value, axis, [(i, (i + steps) % count) for i in range(count)])  47.5 us
    unnamed x14, local copies, waits for them, and re-layouts  6.7 us
    pallas_call x1, Pallas kernels, project(): pl.pallas_call(project_body, grid_spec=pltpu.PrefetchScalarGridSpec(num_s...  6.32 us
    pallas_call x1, Pallas kernels, input_terms(): pl.pallas_call(input_body, grid_spec=pltpu.PrefetchScalarGridSpec(num_sca...  5.9 us
    pallas_call x1, Pallas kernels, attend(): pl.pallas_call(attend_body, grid=(2, 4), in_specs=[wide, wide, head, head...  5.71 us
    pallas_call x2, Pallas kernels, assemble(): pl.pallas_call(body, in_specs=[smem()] + [vmem()] * count + [anywhere] *...  5.24 us
    ppermute x2, starting transfers between devices, down(): return lax.ppermute(value, 's', [(1, 0)])  4.79 us
  transfers between devices with their start and end apart: 39, of which 15 were waited for; matrix products, arithmetic and copies ran while one was open for 0% of the time, Pallas kernels for 13%

profile of v1, /device:TPU:16, one launch (start us, length us, event | category | flops | bytes accessed | tf_op | source)
XLA Modules:
  0.0 180.3 jit_solution(2476146243920311104)
XLA Ops:
  0.7 2.2 %copy-done = bf16[1,4096,512]{2,1,0:T(8,128)(2,1)S(1)} copy-done((bf16[1,4096,512]{2,1,0:T(8,128)(2,1)S(1)}, bf16[1,4096,512]{2,1,0:T(8,128)(2,1)}, u32[]{:S(2)}) %copy-start) | copy-done | bytes 4194328
  2.9 2.2 %copy-done.1 = bf16[1,4096,512]{2,1,0:T(8,128)(2,1)S(1)} copy-done((bf16[1,4096,512]{2,1,0:T(8,128)(2,1)S(1)}, bf16[1,4096,512]{2,1,0:T(8,128)(2,1)}, u32[]{:S(2)}) %copy-start.1) | copy-done | bytes 4194328
  7.4 6.3 %project.1 = (bf16[256,2048]{1,0:T(8,128)(2,1)S(1)}, bf16[256,2048]{1,0:T(8,128)(2,1)S(1)}, f32[256,512]{1,0:T(8,128)S(1)}, f32[256,512]{1,0:T(8,128)S(1)}, f32[256,128]{1,0:T(8,128)S(1)}) custom-call(s32[5]{0:T(128)S(1)} %stack.25.place.refs_0_, bf16[256,4096]{1,0:T(8,128)(2,1)S(1)} %bitcast.17, f32[1,4096]{1,0:T(1,128)S(1)} %copy-done.4, ...), custom_call_target="tpu_custom_call" | custom-call | flops 2147483648 | bytes 12582912 | tf_op jit(solution)/shard_map/project/pallas_call | solution.py:84
  13.9 5.7 %attend.1 = (bf16[256,512]{1,0:T(8,128)(2,1)S(1)}, bf16[256,512]{1,0:T(8,128)(2,1)S(1)}, f32[256,128]{1,0:T(8,128)S(1)}) custom-call(bf16[256,2048]{1,0:T(8,128)(2,1)S(1)} %bitcast.19, bf16[256,2048]{1,0:T(8,128)(2,1)S(1)} %bitcast.20, f32[256,512]{1,0:T(8,128)S(1)} %get-tuple-element.40.kf, f32[256,512]{1,0:T(8,128)S(1)} %get-tuple-element.41.vf), custom_call_target="tpu_custom_call" | custom-call | flops 2400000000 | bytes 4194304 | tf_op jit(solution)/shard_map/attend/pallas_call | solution.py:157
  24.8 2.7 %collective-permute-start.3 = (bf16[512,512]{1,0:T(8,128)(2,1)S(1)}, bf16[512,512]{1,0:T(8,128)(2,1)S(1)}, u32[]{:S(2)}, u32[]{:S(2)}) collective-permute-start(bf16[512,512]{1,0:T(8,128)(2,1)S(1)} %get-tuple-element.45), channel_id=1, source_target_pairs={{0,8},{4,12},{8,0},{12,4},{1,9},{5,13},{9,1},{13,5},{2,10},{6,14},... | collective-permute-start | bytes 1572872 | tf_op jit(solution)/shard_map/ppermute | solution.py:389
  30.8 2.0 %collective-permute-start.9 = (bf16[512,512]{1,0:T(8,128)(2,1)S(1)}, bf16[512,512]{1,0:T(8,128)(2,1)S(1)}, u32[]{:S(2)}, u32[]{:S(2)}) collective-permute-start(bf16[512,512]{1,0:T(8,128)(2,1)S(1)} %get-tuple-element.53), channel_id=1, source_target_pairs={{0,16},{16,32},{32,48},{48,0},{1,17},{17,33},{33,49},{49,1},{2,18}... | collective-permute-start | bytes 1572872 | tf_op jit(solution)/shard_map/ppermute | solution.py:389
  32.8 3.6 %collective-permute-start.10 = (bf16[512,512]{1,0:T(8,128)(2,1)S(1)}, bf16[512,512]{1,0:T(8,128)(2,1)S(1)}, u32[]{:S(2)}, u32[]{:S(2)}) collective-permute-start(bf16[512,512]{1,0:T(8,128)(2,1)S(1)} %get-tuple-element.54), channel_id=1, source_target_pairs={{0,32},{16,48},{32,0},{48,16},{1,33},{17,49},{33,1},{49,17},{2,34}... | collective-permute-start | bytes 1572872 | tf_op jit(solution)/shard_map/ppermute | solution.py:389
  36.4 2.2 %collective-permute-done.2.refs_2_ = bf16[512,512]{1,0:T(8,128)(2,1)S(1)} collective-permute-done((bf16[512,512]{1,0:T(8,128)(2,1)S(1)}, bf16[512,512]{1,0:T(8,128)(2,1)S(1)}, u32[]{:S(2)}, u32[]{:S(2)}) %collective-permute-start.2) | collective-permute-done | bytes 524320 | tf_op jit(solution)/shard_map/ppermute | solution.py:389
  38.6 4.0 %collective-permute-start.11 = (bf16[512,512]{1,0:T(8,128)(2,1)S(1)}, bf16[512,512]{1,0:T(8,128)(2,1)S(1)}, u32[]{:S(2)}, u32[]{:S(2)}) collective-permute-start(bf16[512,512]{1,0:T(8,128)(2,1)S(1)} %get-tuple-element.55), channel_id=1, source_target_pairs={{0,48},{16,0},{32,16},{48,32},{1,49},{17,1},{33,17},{49,33},{2,50}... | collective-permute-start | bytes 1572872 | tf_op jit(solution)/shard_map/ppermute | solution.py:389
  42.6 5.9 %input_terms.1 = (f32[256,4096]{1,0:T(8,128)S(1)}, bf16[128,4096]{1,0:T(8,128)(2,1)S(1)}, bf16[128,4096]{1,0:T(8,128)(2,1)S(1)}) custom-call(s32[5]{0:T(128)S(1)} %stack.25.place.refs_0_, bf16[256,512]{1,0:T(8,128)(2,1)S(1)} %get-tuple-element.51.refs_3_.gk, bf16[256,512]{1,0:T(8,128)(2,1)S(1)} %get-tuple-element.42.refs_3_.gv, ...), custom_call_target="tpu_custom_call" | custom-call | flops 2147483648 | bytes 18874368 | tf_op jit(solution)/shard_map/input_terms/pallas_call | solution.py:214
  48.5 2.3 %collective-permute-done.3.refs_3_ = bf16[512,512]{1,0:T(8,128)(2,1)S(1)} collective-permute-done((bf16[512,512]{1,0:T(8,128)(2,1)S(1)}, bf16[512,512]{1,0:T(8,128)(2,1)S(1)}, u32[]{:S(2)}, u32[]{:S(2)}) %collective-permute-start.3) | collective-permute-done | bytes 524320 | tf_op jit(solution)/shard_map/ppermute | solution.py:389
  50.8 2.3 %collective-permute-start.37 = (bf16[128,4096]{1,0:T(8,128)(2,1)S(1)}, bf16[128,4096]{1,0:T(8,128)(2,1)S(1)}, u32[]{:S(2)}, u32[]{:S(2)}) collective-permute-start(bf16[128,4096]{1,0:T(8,128)(2,1)S(1)} %get-tuple-element.71), channel_id=1, source_target_pairs={{64,0},{65,1},{66,2},{67,3},{68,4},{69,5},{70,6},{71,7},{72,8},{73... | collective-permute-start | bytes 3145736 | tf_op jit(solution)/shard_map/ppermute | solution.py:393
  53.9 2.0 %collective-permute-start.5 = (bf16[128,512]{1,0:T(8,128)(2,1)S(1)}, bf16[128,512]{1,0:T(8,128)(2,1)S(1)}, u32[]{:S(2)}, u32[]{:S(2)}) collective-permute-start(bf16[128,512]{1,0:T(8,128)(2,1)S(1)} %get-tuple-element.48), channel_id=1, source_target_pairs={{0,16},{16,32},{32,48},{48,0},{1,17},{17,33},{33,49},{49,1},{2,18}... | collective-permute-start | bytes 393224 | tf_op jit(solution)/shard_map/ppermute | solution.py:389
  55.9 3.8 %collective-permute-start.6 = (bf16[128,512]{1,0:T(8,128)(2,1)S(1)}, bf16[128,512]{1,0:T(8,128)(2,1)S(1)}, u32[]{:S(2)}, u32[]{:S(2)}) collective-permute-start(bf16[128,512]{1,0:T(8,128)(2,1)S(1)} %get-tuple-element.49), channel_id=1, source_target_pairs={{0,32},{16,48},{32,0},{48,16},{1,33},{17,49},{33,1},{49,17},{2,34}... | collective-permute-start | bytes 393224 | tf_op jit(solution)/shard_map/ppermute | solution.py:389
  66.4 4.0 %collective-permute-done.12.k1 = bf16[128,512]{1,0:T(8,128)(2,1)S(1)} collective-permute-done((bf16[128,512]{1,0:T(8,128)(2,1)S(1)}, bf16[128,512]{1,0:T(8,128)(2,1)S(1)}, u32[]{:S(2)}, u32[]{:S(2)}) %collective-permute-start.12) | collective-permute-done | bytes 131104 | tf_op jit(solution)/shard_map/ppermute | solution.py:389
  72.8 2.5 %collective-permute-start.38 = (bf16[128,4096]{1,0:T(8,128)(2,1)S(1)}, bf16[128,4096]{1,0:T(8,128)(2,1)S(1)}, u32[]{:S(2)}, u32[]{:S(2)}) collective-permute-start(bf16[128,4096]{1,0:T(8,128)(2,1)S(1)} %get-tuple-element.72), channel_id=1, source_target_pairs={{64,0},{65,1},{66,2},{67,3},{68,4},{69,5},{70,6},{71,7},{72,8},{73... | collective-permute-start | bytes 3145736 | tf_op jit(solution)/shard_map/ppermute | solution.py:393
  75.3 6.7 %collective-permute-done.15 = bf16[128,512]{1,0:T(8,128)(2,1)S(1)} collective-permute-done((bf16[128,512]{1,0:T(8,128)(2,1)S(1)}, bf16[128,512]{1,0:T(8,128)(2,1)S(1)}, u32[]{:S(2)}, u32[]{:S(2)}) %collective-permute-start.15) | collective-permute-done | bytes 131104 | tf_op jit(solution)/shard_map/ppermute | solution.py:389
  82.2 23.7 %collective-permute-done.16.other = bf16[128,512]{1,0:T(8,128)(2,1)S(1)} collective-permute-done((bf16[128,512]{1,0:T(8,128)(2,1)S(1)}, bf16[128,512]{1,0:T(8,128)(2,1)S(1)}, u32[]{:S(2)}, u32[]{:S(2)}) %collective-permute-start.16) | collective-permute-done | bytes 131104 | tf_op jit(solution)/shard_map/ppermute | solution.py:389
  108.7 3.0 %collective-permute-done.23.refs_4_ = bf16[128,512]{1,0:T(8,128)(2,1)S(1)} collective-permute-done((bf16[128,512]{1,0:T(8,128)(2,1)S(1)}, bf16[128,512]{1,0:T(8,128)(2,1)S(1)}, u32[]{:S(2)}, u32[]{:S(2)}) %collective-permute-start.23) | collective-permute-done | bytes 131104 | tf_op jit(solution)/shard_map/ppermute | solution.py:389
  111.7 4.0 %collective-permute-start.19 = (bf16[128,512]{1,0:T(8,128)(2,1)S(1)}, bf16[128,512]{1,0:T(8,128)(2,1)S(1)}, u32[]{:S(2)}, u32[]{:S(2)}) collective-permute-start(bf16[128,512]{1,0:T(8,128)(2,1)S(1)} %get-tuple-element.62.refs_1_), channel_id=1, source_target_pairs={{0,48},{16,0},{32,16},{48,32},{1,49},{17,1},{33,17},{49,33},{2,50}... | collective-permute-start | bytes 393224 | tf_op jit(solution)/shard_map/ppermute | solution.py:389
  115.7 2.1 %collective-permute-start.18 = (bf16[128,512]{1,0:T(8,128)(2,1)S(1)}, bf16[128,512]{1,0:T(8,128)(2,1)S(1)}, u32[]{:S(2)}, u32[]{:S(2)}) collective-permute-start(bf16[128,512]{1,0:T(8,128)(2,1)S(1)} %get-tuple-element.62.refs_1_), channel_id=1, source_target_pairs={{0,32},{16,48},{32,0},{48,16},{1,33},{17,49},{33,1},{49,17},{2,34}... | collective-permute-start | bytes 393224 | tf_op jit(solution)/shard_map/ppermute | solution.py:389
  119.9 3.7 %collective-permute-done.18.refs_3_ = bf16[128,512]{1,0:T(8,128)(2,1)S(1)} collective-permute-done((bf16[128,512]{1,0:T(8,128)(2,1)S(1)}, bf16[128,512]{1,0:T(8,128)(2,1)S(1)}, u32[]{:S(2)}, u32[]{:S(2)}) %collective-permute-start.18) | collective-permute-done | bytes 131104 | tf_op jit(solution)/shard_map/ppermute | solution.py:389
  123.6 2.1 %collective-permute-start.28 = (bf16[512,512]{1,0:T(8,128)(2,1)S(1)}, bf16[512,512]{1,0:T(8,128)(2,1)S(1)}, u32[]{:S(2)}, u32[]{:S(2)}) collective-permute-start(bf16[512,512]{1,0:T(8,128)(2,1)S(1)} %stack.27.refs_2_), channel_id=1, source_target_pairs={{0,32},{16,48},{32,0},{48,16},{1,33},{17,49},{33,1},{49,17},{2,34}... | collective-permute-start | bytes 1572872 | tf_op jit(solution)/shard_map/ppermute | solution.py:389
  127.7 9.4 %collective-permute-done.34.refs_6_ = bf16[512,512]{1,0:T(8,128)(2,1)S(1)} collective-permute-done((bf16[512,512]{1,0:T(8,128)(2,1)S(1)}, bf16[512,512]{1,0:T(8,128)(2,1)S(1)}, u32[]{:S(2)}, u32[]{:S(2)}) %collective-permute-start.34) | collective-permute-done | bytes 524320 | tf_op jit(solution)/shard_map/ppermute | solution.py:389
  137.1 2.2 %collective-permute-start.27 = (bf16[512,512]{1,0:T(8,128)(2,1)S(1)}, bf16[512,512]{1,0:T(8,128)(2,1)S(1)}, u32[]{:S(2)}, u32[]{:S(2)}) collective-permute-start(bf16[512,512]{1,0:T(8,128)(2,1)S(1)} %stack.26.refs_1_), channel_id=1, source_target_pairs={{0,8},{4,12},{8,0},{12,4},{1,9},{5,13},{9,1},{13,5},{2,10},{6,14},... | collective-permute-start | bytes 1572872 | tf_op jit(solution)/shard_map/ppermute | solution.py:389
  139.2 5.7 %collective-permute-done.28.refs_6_ = bf16[512,512]{1,0:T(8,128)(2,1)S(1)} collective-permute-done((bf16[512,512]{1,0:T(8,128)(2,1)S(1)}, bf16[512,512]{1,0:T(8,128)(2,1)S(1)}, u32[]{:S(2)}, u32[]{:S(2)}) %collective-permute-start.28) | collective-permute-done | bytes 524320 | tf_op jit(solution)/shard_map/ppermute | solution.py:389
  144.9 4.7 %collective-permute-start.20 = (bf16[512,512]{1,0:T(8,128)(2,1)S(1)}, bf16[512,512]{1,0:T(8,128)(2,1)S(1)}, u32[]{:S(2)}, u32[]{:S(2)}) collective-permute-start(bf16[512,512]{1,0:T(8,128)(2,1)S(1)} %stack.26.refs_1_), channel_id=1, source_target_pairs={{0,12},{4,0},{8,4},{12,8},{1,13},{5,1},{9,5},{13,9},{2,14},{6,2},{... | collective-permute-start | bytes 1572872 | tf_op jit(solution)/shard_map/ppermute | solution.py:389
  150.3 2.7 %collective-permute-done.27.refs_5_ = bf16[512,512]{1,0:T(8,128)(2,1)S(1)} collective-permute-done((bf16[512,512]{1,0:T(8,128)(2,1)S(1)}, bf16[512,512]{1,0:T(8,128)(2,1)S(1)}, u32[]{:S(2)}, u32[]{:S(2)}) %collective-permute-start.27) | collective-permute-done | bytes 524320 | tf_op jit(solution)/shard_map/ppermute | solution.py:389
  152.9 17.9 %collective-permute-done.20.refs_1_ = bf16[512,512]{1,0:T(8,128)(2,1)S(1)} collective-permute-done((bf16[512,512]{1,0:T(8,128)(2,1)S(1)}, bf16[512,512]{1,0:T(8,128)(2,1)S(1)}, u32[]{:S(2)}, u32[]{:S(2)}) %collective-permute-start.20) | collective-permute-done | bytes 524320 | tf_op jit(solution)/shard_map/ppermute | solution.py:389
  171.4 3.4 %finish.1 = bf16[256,4096]{1,0:T(8,128)(2,1)} custom-call(f32[256,4096]{1,0:T(8,128)S(1)} %get-tuple-element.70.own, bf16[128,4096]{1,0:T(8,128)(2,1)S(1)} %collective-permute-done.37.lower, bf16[128,4096]{1,0:T(8,128)(2,1)S(1)} %collective-permute-done.38.upper), custom_call_target="tpu_custom_call" | custom-call | flops 1048576 | bytes 8388608 | tf_op jit(solution)/shard_map/finish/pallas_call | solution.py:252
  174.8 2.6 %assemble.2 = (bf16[4096,512]{1,0:T(8,128)(2,1)}, bf16[4096,512]{1,0:T(8,128)(2,1)}) custom-call(s32[5]{0:T(128)S(1)} %stack.25.place.refs_0_, bf16[512,512]{1,0:T(8,128)(2,1)S(1)} %stack.26.refs_1_, bf16[512,512]{1,0:T(8,128)(2,1)S(1)} %stack.27.refs_2_, bf16[512,512]{1,0:T(8,128)(2,1)S(1)} %collective-permute-done.31.refs_3_, ...), custom_call_target="tpu_custom_call" | custom-call | tf_op jit(solution)/shard_map/assemble/pallas_call | solution.py:375
  177.5 2.6 %assemble.3 = (bf16[4096,512]{1,0:T(8,128)(2,1)}, bf16[4096,512]{1,0:T(8,128)(2,1)}) custom-call(s32[5]{0:T(128)S(1)} %stack.25.place.refs_0_, bf16[512,512]{1,0:T(8,128)(2,1)S(1)} %collective-permute-done.20.refs_1_, bf16[512,512]{1,0:T(8,128)(2,1)S(1)} %collective-permute-done.24.refs_2_, ...), custom_call_target="tpu_custom_call", output_to_operand_aliasing={{0}: (9, {}), {1}: (10, {})} | custom-call | tf_op jit(solution)/shard_map/assemble/pallas_call | solution.py:375
  (76 shorter events, 29.0 us)
Async XLA Ops:
  13.7 7.5 %collective-permute-start = (bf16[256,2048]{1,0:T(8,128)(2,1)S(1)}, bf16[256,2048]{1,0:T(8,128)(2,1)S(1)}, u32[]{:S(2)}, u32[]{:S(2)}) collective-permute-start(bf16[256,2048]{1,0:T(8,128)(2,1)S(1)} %get-tuple-element.39), channel_id=1, source_target_pairs={{0,1},{1,0},{2,3},{3,2},{4,5},{5,4},{6,7},{7,6},{8,9},{9,8},{10,11... | collective-permute-start | bytes 3145736 | tf_op jit(solution)/shard_map/ppermute | solution.py:389
  23.1 15.5 %collective-permute-start.2 = (bf16[512,512]{1,0:T(8,128)(2,1)S(1)}, bf16[512,512]{1,0:T(8,128)(2,1)S(1)}, u32[]{:S(2)}, u32[]{:S(2)}) collective-permute-start(bf16[512,512]{1,0:T(8,128)(2,1)S(1)} %get-tuple-element.44), channel_id=1, source_target_pairs={{0,4},{4,8},{8,12},{12,0},{1,5},{5,9},{9,13},{13,1},{2,6},{6,10},{... | collective-permute-start | bytes 1572872 | tf_op jit(solution)/shard_map/ppermute | solution.py:389
  24.8 26.1 %collective-permute-start.3 = (bf16[512,512]{1,0:T(8,128)(2,1)S(1)}, bf16[512,512]{1,0:T(8,128)(2,1)S(1)}, u32[]{:S(2)}, u32[]{:S(2)}) collective-permute-start(bf16[512,512]{1,0:T(8,128)(2,1)S(1)} %get-tuple-element.45), channel_id=1, source_target_pairs={{0,8},{4,12},{8,0},{12,4},{1,9},{5,13},{9,1},{13,5},{2,10},{6,14},... | collective-permute-start | bytes 1572872 | tf_op jit(solution)/shard_map/ppermute | solution.py:389
  27.5 25.6 %collective-permute-start.4 = (bf16[512,512]{1,0:T(8,128)(2,1)S(1)}, bf16[512,512]{1,0:T(8,128)(2,1)S(1)}, u32[]{:S(2)}, u32[]{:S(2)}) collective-permute-start(bf16[512,512]{1,0:T(8,128)(2,1)S(1)} %get-tuple-element.46), channel_id=1, source_target_pairs={{0,12},{4,0},{8,4},{12,8},{1,13},{5,1},{9,5},{13,9},{2,14},{6,2},{... | collective-permute-start | bytes 1572872 | tf_op jit(solution)/shard_map/ppermute | solution.py:389
  30.8 25.1 %collective-permute-start.9 = (bf16[512,512]{1,0:T(8,128)(2,1)S(1)}, bf16[512,512]{1,0:T(8,128)(2,1)S(1)}, u32[]{:S(2)}, u32[]{:S(2)}) collective-permute-start(bf16[512,512]{1,0:T(8,128)(2,1)S(1)} %get-tuple-element.53), channel_id=1, source_target_pairs={{0,16},{16,32},{32,48},{48,0},{1,17},{17,33},{33,49},{49,1},{2,18}... | collective-permute-start | bytes 1572872 | tf_op jit(solution)/shard_map/ppermute | solution.py:389
  32.8 26.9 %collective-permute-start.10 = (bf16[512,512]{1,0:T(8,128)(2,1)S(1)}, bf16[512,512]{1,0:T(8,128)(2,1)S(1)}, u32[]{:S(2)}, u32[]{:S(2)}) collective-permute-start(bf16[512,512]{1,0:T(8,128)(2,1)S(1)} %get-tuple-element.54), channel_id=1, source_target_pairs={{0,32},{16,48},{32,0},{48,16},{1,33},{17,49},{33,1},{49,17},{2,34}... | collective-permute-start | bytes 1572872 | tf_op jit(solution)/shard_map/ppermute | solution.py:389
  38.6 21.9 %collective-permute-start.11 = (bf16[512,512]{1,0:T(8,128)(2,1)S(1)}, bf16[512,512]{1,0:T(8,128)(2,1)S(1)}, u32[]{:S(2)}, u32[]{:S(2)}) collective-permute-start(bf16[512,512]{1,0:T(8,128)(2,1)S(1)} %get-tuple-element.55), channel_id=1, source_target_pairs={{0,48},{16,0},{32,16},{48,32},{1,49},{17,1},{33,17},{49,33},{2,50}... | collective-permute-start | bytes 1572872 | tf_op jit(solution)/shard_map/ppermute | solution.py:389
  50.8 68.6 %collective-permute-start.37 = (bf16[128,4096]{1,0:T(8,128)(2,1)S(1)}, bf16[128,4096]{1,0:T(8,128)(2,1)S(1)}, u32[]{:S(2)}, u32[]{:S(2)}) collective-permute-start(bf16[128,4096]{1,0:T(8,128)(2,1)S(1)} %get-tuple-element.71), channel_id=1, source_target_pairs={{64,0},{65,1},{66,2},{67,3},{68,4},{69,5},{70,6},{71,7},{72,8},{73... | collective-permute-start | bytes 3145736 | tf_op jit(solution)/shard_map/ppermute | solution.py:393
  53.9 9.6 %collective-permute-start.5 = (bf16[128,512]{1,0:T(8,128)(2,1)S(1)}, bf16[128,512]{1,0:T(8,128)(2,1)S(1)}, u32[]{:S(2)}, u32[]{:S(2)}) collective-permute-start(bf16[128,512]{1,0:T(8,128)(2,1)S(1)} %get-tuple-element.48), channel_id=1, source_target_pairs={{0,16},{16,32},{32,48},{48,0},{1,17},{17,33},{33,49},{49,1},{2,18}... | collective-permute-start | bytes 393224 | tf_op jit(solution)/shard_map/ppermute | solution.py:389
  55.9 9.0 %collective-permute-start.6 = (bf16[128,512]{1,0:T(8,128)(2,1)S(1)}, bf16[128,512]{1,0:T(8,128)(2,1)S(1)}, u32[]{:S(2)}, u32[]{:S(2)}) collective-permute-start(bf16[128,512]{1,0:T(8,128)(2,1)S(1)} %get-tuple-element.49), channel_id=1, source_target_pairs={{0,32},{16,48},{32,0},{48,16},{1,33},{17,49},{33,1},{49,17},{2,34}... | collective-permute-start | bytes 393224 | tf_op jit(solution)/shard_map/ppermute | solution.py:389
  61.3 9.1 %collective-permute-start.12 = (bf16[128,512]{1,0:T(8,128)(2,1)S(1)}, bf16[128,512]{1,0:T(8,128)(2,1)S(1)}, u32[]{:S(2)}, u32[]{:S(2)}) collective-permute-start(bf16[128,512]{1,0:T(8,128)(2,1)S(1)} %get-tuple-element.57), channel_id=1, source_target_pairs={{0,4},{4,8},{8,12},{12,0},{1,5},{5,9},{9,13},{13,1},{2,6},{6,10},{... | collective-permute-start | bytes 393224 | tf_op jit(solution)/shard_map/ppermute | solution.py:389
  63.5 6.9 %collective-permute-start.13 = (bf16[128,512]{1,0:T(8,128)(2,1)S(1)}, bf16[128,512]{1,0:T(8,128)(2,1)S(1)}, u32[]{:S(2)}, u32[]{:S(2)}) collective-permute-start(bf16[128,512]{1,0:T(8,128)(2,1)S(1)} %get-tuple-element.58), channel_id=1, source_target_pairs={{0,8},{4,12},{8,0},{12,4},{1,9},{5,13},{9,1},{13,5},{2,10},{6,14},... | collective-permute-start | bytes 393224 | tf_op jit(solution)/shard_map/ppermute | solution.py:389
  71.0 11.0 %collective-permute-start.15 = (bf16[128,512]{1,0:T(8,128)(2,1)S(1)}, bf16[128,512]{1,0:T(8,128)(2,1)S(1)}, u32[]{:S(2)}, u32[]{:S(2)}) collective-permute-start(bf16[128,512]{1,0:T(8,128)(2,1)S(1)} %get-tuple-element.61), channel_id=1, source_target_pairs={{0,2},{2,0},{1,3},{3,1},{4,6},{6,4},{5,7},{7,5},{8,10},{10,8},{9,1... | collective-permute-start | bytes 393224 | tf_op jit(solution)/shard_map/ppermute | solution.py:389
  72.8 54.8 %collective-permute-start.38 = (bf16[128,4096]{1,0:T(8,128)(2,1)S(1)}, bf16[128,4096]{1,0:T(8,128)(2,1)S(1)}, u32[]{:S(2)}, u32[]{:S(2)}) collective-permute-start(bf16[128,4096]{1,0:T(8,128)(2,1)S(1)} %get-tuple-element.72), channel_id=1, source_target_pairs={{64,0},{65,1},{66,2},{67,3},{68,4},{69,5},{70,6},{71,7},{72,8},{73... | collective-permute-start | bytes 3145736 | tf_op jit(solution)/shard_map/ppermute | solution.py:393
  82.1 23.8 %collective-permute-start.16 = (bf16[128,512]{1,0:T(8,128)(2,1)S(1)}, bf16[128,512]{1,0:T(8,128)(2,1)S(1)}, u32[]{:S(2)}, u32[]{:S(2)}) collective-permute-start(bf16[128,512]{1,0:T(8,128)(2,1)S(1)} %multiply_convert_fusion.block), channel_id=1, source_target_pairs={{0,2},{2,0},{1,3},{3,1},{4,6},{6,4},{5,7},{7,5},{8,10},{10,8},{9,1... | collective-permute-start | bytes 393224 | tf_op jit(solution)/shard_map/ppermute | solution.py:389
  106.5 9.2 %collective-permute-start.22 = (bf16[128,512]{1,0:T(8,128)(2,1)S(1)}, bf16[128,512]{1,0:T(8,128)(2,1)S(1)}, u32[]{:S(2)}, u32[]{:S(2)}) collective-permute-start(bf16[128,512]{1,0:T(8,128)(2,1)S(1)} %get-tuple-element.63.refs_1_), channel_id=1, source_target_pairs={{0,8},{4,12},{8,0},{12,4},{1,9},{5,13},{9,1},{13,5},{2,10},{6,14},... | collective-permute-start | bytes 393224 | tf_op jit(solution)/shard_map/ppermute | solution.py:389
  107.4 10.4 %collective-permute-start.21 = (bf16[128,512]{1,0:T(8,128)(2,1)S(1)}, bf16[128,512]{1,0:T(8,128)(2,1)S(1)}, u32[]{:S(2)}, u32[]{:S(2)}) collective-permute-start(bf16[128,512]{1,0:T(8,128)(2,1)S(1)} %get-tuple-element.63.refs_1_), channel_id=1, source_target_pairs={{0,4},{4,8},{8,12},{12,0},{1,5},{5,9},{9,13},{13,1},{2,6},{6,10},{... | collective-permute-start | bytes 393224 | tf_op jit(solution)/shard_map/ppermute | solution.py:389
  111.7 8.2 %collective-permute-start.19 = (bf16[128,512]{1,0:T(8,128)(2,1)S(1)}, bf16[128,512]{1,0:T(8,128)(2,1)S(1)}, u32[]{:S(2)}, u32[]{:S(2)}) collective-permute-start(bf16[128,512]{1,0:T(8,128)(2,1)S(1)} %get-tuple-element.62.refs_1_), channel_id=1, source_target_pairs={{0,48},{16,0},{32,16},{48,32},{1,49},{17,1},{33,17},{49,33},{2,50}... | collective-permute-start | bytes 393224 | tf_op jit(solution)/shard_map/ppermute | solution.py:389
  115.7 7.9 %collective-permute-start.18 = (bf16[128,512]{1,0:T(8,128)(2,1)S(1)}, bf16[128,512]{1,0:T(8,128)(2,1)S(1)}, u32[]{:S(2)}, u32[]{:S(2)}) collective-permute-start(bf16[128,512]{1,0:T(8,128)(2,1)S(1)} %get-tuple-element.62.refs_1_), channel_id=1, source_target_pairs={{0,32},{16,48},{32,0},{48,16},{1,33},{17,49},{33,1},{49,17},{2,34}... | collective-permute-start | bytes 393224 | tf_op jit(solution)/shard_map/ppermute | solution.py:389
  117.8 8.1 %collective-permute-start.17 = (bf16[128,512]{1,0:T(8,128)(2,1)S(1)}, bf16[128,512]{1,0:T(8,128)(2,1)S(1)}, u32[]{:S(2)}, u32[]{:S(2)}) collective-permute-start(bf16[128,512]{1,0:T(8,128)(2,1)S(1)} %get-tuple-element.62.refs_1_), channel_id=1, source_target_pairs={{0,16},{16,32},{32,48},{48,0},{1,17},{17,33},{33,49},{49,1},{2,18}... | collective-permute-start | bytes 393224 | tf_op jit(solution)/shard_map/ppermute | solution.py:389
  119.4 17.6 %collective-permute-start.34 = (bf16[512,512]{1,0:T(8,128)(2,1)S(1)}, bf16[512,512]{1,0:T(8,128)(2,1)S(1)}, u32[]{:S(2)}, u32[]{:S(2)}) collective-permute-start(bf16[512,512]{1,0:T(8,128)(2,1)S(1)} %stack.27.refs_2_), channel_id=1, source_target_pairs={{0,16},{16,32},{32,48},{48,0},{1,17},{17,33},{33,49},{49,1},{2,18}... | collective-permute-start | bytes 1572872 | tf_op jit(solution)/shard_map/ppermute | solution.py:389
  119.9 17.2 %collective-permute-start.32 = (bf16[512,512]{1,0:T(8,128)(2,1)S(1)}, bf16[512,512]{1,0:T(8,128)(2,1)S(1)}, u32[]{:S(2)}, u32[]{:S(2)}) collective-permute-start(bf16[512,512]{1,0:T(8,128)(2,1)S(1)} %stack.27.refs_2_), channel_id=1, source_target_pairs={{0,1},{1,0},{2,3},{3,2},{4,5},{5,4},{6,7},{7,6},{8,9},{9,8},{10,11... | collective-permute-start | bytes 1572872 | tf_op jit(solution)/shard_map/ppermute | solution.py:389
  123.6 21.3 %collective-permute-start.28 = (bf16[512,512]{1,0:T(8,128)(2,1)S(1)}, bf16[512,512]{1,0:T(8,128)(2,1)S(1)}, u32[]{:S(2)}, u32[]{:S(2)}) collective-permute-start(bf16[512,512]{1,0:T(8,128)(2,1)S(1)} %stack.27.refs_2_), channel_id=1, source_target_pairs={{0,32},{16,48},{32,0},{48,16},{1,33},{17,49},{33,1},{49,17},{2,34}... | collective-permute-start | bytes 1572872 | tf_op jit(solution)/shard_map/ppermute | solution.py:389
  125.9 23.8 %collective-permute-start.24 = (bf16[512,512]{1,0:T(8,128)(2,1)S(1)}, bf16[512,512]{1,0:T(8,128)(2,1)S(1)}, u32[]{:S(2)}, u32[]{:S(2)}) collective-permute-start(bf16[512,512]{1,0:T(8,128)(2,1)S(1)} %stack.27.refs_2_), channel_id=1, source_target_pairs={{0,48},{16,0},{32,16},{48,32},{1,49},{17,1},{33,17},{49,33},{2,50}... | collective-permute-start | bytes 1572872 | tf_op jit(solution)/shard_map/ppermute | solution.py:389
  127.6 22.1 %collective-permute-start.33 = (bf16[512,512]{1,0:T(8,128)(2,1)S(1)}, bf16[512,512]{1,0:T(8,128)(2,1)S(1)}, u32[]{:S(2)}, u32[]{:S(2)}) collective-permute-start(bf16[512,512]{1,0:T(8,128)(2,1)S(1)} %stack.26.refs_1_), channel_id=1, source_target_pairs={{0,4},{4,8},{8,12},{12,0},{1,5},{5,9},{9,13},{13,1},{2,6},{6,10},{... | collective-permute-start | bytes 1572872 | tf_op jit(solution)/shard_map/ppermute | solution.py:389
  137.1 13.1 %collective-permute-start.31 = (bf16[512,512]{1,0:T(8,128)(2,1)S(1)}, bf16[512,512]{1,0:T(8,128)(2,1)S(1)}, u32[]{:S(2)}, u32[]{:S(2)}) collective-permute-start(bf16[512,512]{1,0:T(8,128)(2,1)S(1)} %stack.26.refs_1_), channel_id=1, source_target_pairs={{0,1},{1,0},{2,3},{3,2},{4,5},{5,4},{6,7},{7,6},{8,9},{9,8},{10,11... | collective-permute-start | bytes 1572872 | tf_op jit(solution)/shard_map/ppermute | solution.py:389
  137.1 15.8 %collective-permute-start.27 = (bf16[512,512]{1,0:T(8,128)(2,1)S(1)}, bf16[512,512]{1,0:T(8,128)(2,1)S(1)}, u32[]{:S(2)}, u32[]{:S(2)}) collective-permute-start(bf16[512,512]{1,0:T(8,128)(2,1)S(1)} %stack.26.refs_1_), channel_id=1, source_target_pairs={{0,8},{4,12},{8,0},{12,4},{1,9},{5,13},{9,1},{13,5},{2,10},{6,14},... | collective-permute-start | bytes 1572872 | tf_op jit(solution)/shard_map/ppermute | solution.py:389
  144.9 25.9 %collective-permute-start.20 = (bf16[512,512]{1,0:T(8,128)(2,1)S(1)}, bf16[512,512]{1,0:T(8,128)(2,1)S(1)}, u32[]{:S(2)}, u32[]{:S(2)}) collective-permute-start(bf16[512,512]{1,0:T(8,128)(2,1)S(1)} %stack.26.refs_1_), channel_id=1, source_target_pairs={{0,12},{4,0},{8,4},{12,8},{1,13},{5,1},{9,5},{13,9},{2,14},{6,2},{... | collective-permute-start | bytes 1572872 | tf_op jit(solution)/shard_map/ppermute | solution.py:389
  149.7 21.2 %collective-permute-start.36 = (bf16[512,512]{1,0:T(8,128)(2,1)S(1)}, bf16[512,512]{1,0:T(8,128)(2,1)S(1)}, u32[]{:S(2)}, u32[]{:S(2)}) collective-permute-start(bf16[512,512]{1,0:T(8,128)(2,1)S(1)} %collective-permute-done.34.refs_6_), channel_id=1, source_target_pairs={{0,1},{1,0},{2,3},{3,2},{4,5},{5,4},{6,7},{7,6},{8,9},{9,8},{10,11... | collective-permute-start | bytes 1572872 | tf_op jit(solution)/shard_map/ppermute | solution.py:389
  149.7 27.8 %collective-permute-start.30 = (bf16[512,512]{1,0:T(8,128)(2,1)S(1)}, bf16[512,512]{1,0:T(8,128)(2,1)S(1)}, u32[]{:S(2)}, u32[]{:S(2)}) collective-permute-start(bf16[512,512]{1,0:T(8,128)(2,1)S(1)} %collective-permute-done.28.refs_6_), channel_id=1, source_target_pairs={{0,1},{1,0},{2,3},{3,2},{4,5},{5,4},{6,7},{7,6},{8,9},{9,8},{10,11... | collective-permute-start | bytes 1572872 | tf_op jit(solution)/shard_map/ppermute | solution.py:389
  150.2 24.6 %collective-permute-start.35 = (bf16[512,512]{1,0:T(8,128)(2,1)S(1)}, bf16[512,512]{1,0:T(8,128)(2,1)S(1)}, u32[]{:S(2)}, u32[]{:S(2)}) collective-permute-start(bf16[512,512]{1,0:T(8,128)(2,1)S(1)} %collective-permute-done.33.refs_5_), channel_id=1, source_target_pairs={{0,1},{1,0},{2,3},{3,2},{4,5},{5,4},{6,7},{7,6},{8,9},{9,8},{10,11... | collective-permute-start | bytes 1572872 | tf_op jit(solution)/shard_map/ppermute | solution.py:389
  152.9 24.5 %collective-permute-start.26 = (bf16[512,512]{1,0:T(8,128)(2,1)S(1)}, bf16[512,512]{1,0:T(8,128)(2,1)S(1)}, u32[]{:S(2)}, u32[]{:S(2)}) collective-permute-start(bf16[512,512]{1,0:T(8,128)(2,1)S(1)} %collective-permute-done.24.refs_2_), channel_id=1, source_target_pairs={{0,1},{1,0},{2,3},{3,2},{4,5},{5,4},{6,7},{7,6},{8,9},{9,8},{10,11... | collective-permute-start | bytes 1572872 | tf_op jit(solution)/shard_map/ppermute | solution.py:389
  (14 other events, 79.2 us)

commit v2 on v1

v2 whole, which is shorter than its diff:
```python
import jax
import jax.numpy as jnp
from jax import lax
from jax.experimental import pallas as pl
from jax.experimental.pallas import tpu as pltpu
from jax.sharding import Mesh
from jax.sharding import PartitionSpec as P

HEAD = 128
WIDTH = 4096
COLS = 512
ROWS = 256
REPLICAS = 64
epsilon = 1e-05
SCALE = HEAD ** (-0.5)


bf16 = jnp.bfloat16
f32 = jnp.float32


def shape(dims, dtype):
    return jax.ShapeDtypeStruct(dims, dtype)


def vmem():
    return pl.BlockSpec(memory_space=pltpu.VMEM)


def held(dims, dtype):
    return pltpu.VMEM(dims, dtype)


def hold(*arrays):
    return tuple(pltpu.with_memory_space_constraint(a, pltpu.VMEM) for a in arrays)


def smem():
    return pl.BlockSpec(memory_space=pltpu.SMEM)


def far(*arrays):
    return tuple(pltpu.with_memory_space_constraint(a, pltpu.HBM) for a in arrays)


def budget(mebibytes):
    return pltpu.CompilerParams(vmem_limit_bytes=mebibytes << 20)


def project_body(place, x, gain, wk, wv, send, mine, keys, values, inverse, acc_k, acc_v, inv):
    step = pl.program_id(0)
    tile = (step + 2 * (1 - place[3])) % 4

    @pl.when(step == 0)
    def _():
        total = jnp.zeros((ROWS, 128), f32)
        for i in range(WIDTH // 128):
            part = x[:, i * 128 : (i + 1) * 128].astype(f32)
            total = total + part * part
        mean = jnp.sum(total, axis=1, keepdims=True) / WIDTH
        inv[...] = jnp.broadcast_to(lax.rsqrt(mean + epsilon), (ROWS, 128))
        inverse[...] = inv[...]
        acc_k[...] = jnp.zeros_like(acc_k)
        acc_v[...] = jnp.zeros_like(acc_v)

    part = x[:, pl.ds(pl.multiple_of(tile * 1024, 1024), 1024)].astype(f32)
    normed = (part * inv[:, :1] * gain[...]).astype(bf16)

    @pl.when(step < 2)
    def _():
        send[...] = normed

    @pl.when(step >= 2)
    def _():
        mine[...] = normed

    acc_k[...] += jnp.dot(normed, wk[...], preferred_element_type=f32)
    acc_v[...] += jnp.dot(normed, wv[...], preferred_element_type=f32)

    @pl.when(step == 3)
    def _():
        keys[...] = acc_k[...]
        values[...] = acc_v[...]


def project(place, x, gain, wk, wv):
    tile = lambda i, p: (i + 2 * (1 - p[3])) % 4
    return pl.pallas_call(
        project_body,
        grid_spec=pltpu.PrefetchScalarGridSpec(
            num_scalar_prefetch=1,
            grid=(4,),
            in_specs=[
                pl.BlockSpec((ROWS, WIDTH), lambda i, p: (0, 0)),
                pl.BlockSpec((1, 1024), lambda i, p: (0, tile(i, p))),
                pl.BlockSpec((1024, COLS), lambda i, p: (tile(i, p), 0)),
                pl.BlockSpec((1024, COLS), lambda i, p: (tile(i, p), 0)),
            ],
            out_specs=[
                pl.BlockSpec((ROWS, 1024), lambda i, p: (0, jnp.minimum(i, 1))),
                pl.BlockSpec((ROWS, 1024), lambda i, p: (0, jnp.maximum(i - 2, 0))),
                pl.BlockSpec((ROWS, COLS), lambda i, p: (0, 0)),
                pl.BlockSpec((ROWS, COLS), lambda i, p: (0, 0)),
                pl.BlockSpec((ROWS, 128), lambda i, p: (0, 0)),
            ],
            scratch_shapes=[
                pltpu.VMEM((ROWS, COLS), f32),
                pltpu.VMEM((ROWS, COLS), f32),
                pltpu.VMEM((ROWS, 128), f32),
            ],
        ),
        out_shape=[
            shape((ROWS, 2048), bf16),
            shape((ROWS, 2048), bf16),
            shape((ROWS, COLS), f32),
            shape((ROWS, COLS), f32),
            shape((ROWS, 128), f32),
        ],
        cost_estimate=pl.CostEstimate(flops=2 * ROWS * WIDTH * 1024, bytes_accessed=12 << 20, transcendentals=0),
        name="project",
        compiler_params=budget(24),
    )(place, *far(x), gain, *far(wk, wv))


def attend_body(q, og, kf, vf, gk, gv, row):
    def heads(ref):
        return jnp.concatenate([ref[:, h * HEAD : (h + 1) * HEAD] for h in range(4)], axis=0)

    nt = (((1,), (1,)), ((), ()))
    q4 = heads(q)
    g4 = heads(og)
    key = kf[...]
    value = vf[...]
    scores = lax.dot_general(key.astype(bf16), q4, nt, preferred_element_type=f32) * SCALE
    key_at = lax.broadcasted_iota(jnp.int32, (HEAD, 512), 0)
    query_at = lax.broadcasted_iota(jnp.int32, (HEAD, 512), 1) & (HEAD - 1)
    scores = jnp.where(key_at <= query_at, scores, -1e30)
    weight = jnp.exp(scores - jnp.max(scores, axis=0, keepdims=True))
    prob = weight / jnp.sum(weight, axis=0, keepdims=True)
    grad_value = jnp.dot(prob.astype(bf16), g4, preferred_element_type=f32).astype(bf16)
    grad_prob = lax.dot_general(value.astype(bf16), g4, nt, preferred_element_type=f32)
    delta = jnp.sum(prob * grad_prob, axis=0, keepdims=True)
    dscore = (prob * (grad_prob - delta) * SCALE).astype(bf16)
    grad_key = jnp.dot(dscore, q4, preferred_element_type=f32).astype(bf16)
    gk[...] = grad_key
    gv[...] = grad_value
    term = grad_key.astype(f32) * key + grad_value.astype(f32) * value

    @pl.when(pl.program_id(1) == 0)
    def _():
        row[...] = term

    @pl.when(pl.program_id(1) != 0)
    def _():
        row[...] += term


def attend(q, og, kf, vf):
    wide = pl.BlockSpec((128, 512), lambda s, j: (s, j))
    head = pl.BlockSpec((128, 128), lambda s, j: (s, j))
    return pl.pallas_call(
        attend_body,
        grid=(2, 4),
        in_specs=[wide, wide, head, head],
        out_specs=[head, head, pl.BlockSpec((128, 128), lambda s, j: (s, 0))],
        out_shape=[shape((ROWS, COLS), bf16), shape((ROWS, COLS), bf16), shape((ROWS, 128), f32)],
        cost_estimate=pl.CostEstimate(flops=600_000_000 * 4, bytes_accessed=4 << 20, transcendentals=1 << 19),
        name="attend",
        compiler_params=budget(16),
    )(q, og, kf, vf)


def weight_chunk(place, mine, theirs, grad, grad_theirs, axis, k):
    tn = (((0,), (0,)), ((), ()))
    start = pl.multiple_of(((place[axis] + k) % 4) * 512, 512)
    part = lax.dot_general(mine[:, pl.ds(start, 512)], grad[...], tn, preferred_element_type=f32)
    return part + lax.dot_general(
        theirs[:, pl.ds(start, 512)], grad_theirs[...], tn, preferred_element_type=f32
    )


def weight_far_body(place, mine, theirs, grad, grad_theirs, top, bottom, *, axis):
    part = weight_chunk(place, mine, theirs, grad, grad_theirs, axis, 2).astype(bf16)
    top[...] = part[:256]
    bottom[...] = part[256:]


def weight_far(place, mine, theirs, grad, grad_theirs, axis):
    return pl.pallas_call(
        lambda *refs: weight_far_body(*refs, axis=axis),
        in_specs=[smem()] + [vmem()] * 4,
        out_specs=[vmem()] * 2,
        out_shape=[held((256, COLS), bf16)] * 2,
        cost_estimate=pl.CostEstimate(flops=2 * 512 * 512 * 512, bytes_accessed=2 << 20, transcendentals=0),
        name="weight_far",
        compiler_params=budget(8),
    )(place, *hold(mine, theirs, grad, grad_theirs))


def weight_near_body(place, mine, theirs, grad, grad_theirs, own, ahead, behind, *, axis):
    for k, ref in ((1, ahead), (3, behind), (0, own)):
        ref[...] = weight_chunk(place, mine, theirs, grad, grad_theirs, axis, k)


def weight_near(place, mine, theirs, grad, grad_theirs, axis):
    return pl.pallas_call(
        lambda *refs: weight_near_body(*refs, axis=axis),
        in_specs=[smem()] + [vmem()] * 4,
        out_specs=[vmem()] * 3,
        out_shape=[held((512, COLS), f32)] * 3,
        cost_estimate=pl.CostEstimate(flops=6 * 512 * 512 * 512, bytes_accessed=5 << 20, transcendentals=0),
        name="weight_near",
        compiler_params=budget(8),
    )(place, *hold(mine, theirs, grad, grad_theirs))


def relay_body(ahead, behind, top, bottom, to_ahead, to_behind):
    to_ahead[:256, :] = (ahead[:256, :] + top[...].astype(f32)).astype(bf16)
    to_ahead[256:, :] = ahead[256:, :].astype(bf16)
    to_behind[:256, :] = behind[:256, :].astype(bf16)
    to_behind[256:, :] = (behind[256:, :] + bottom[...].astype(f32)).astype(bf16)


def relay(ahead, behind, top, bottom):
    return pl.pallas_call(
        relay_body,
        in_specs=[vmem()] * 4,
        out_specs=[vmem()] * 2,
        out_shape=[held((512, COLS), bf16)] * 2,
        name="relay",
        compiler_params=budget(4),
    )(*hold(ahead, behind, top, bottom))


def input_body(place, gk, gv, wk, wv, x, top, gain, inverse, row, own, lower, upper):
    nt = (((1,), (1,)), ((), ()))
    grad_norm = lax.dot_general(gk[...], wk[...], nt, preferred_element_type=f32)
    grad_norm = grad_norm + lax.dot_general(gv[...], wv[...], nt, preferred_element_type=f32)
    inv = inverse[:, :1]
    mean = jnp.sum(row[...], axis=1, keepdims=True) * (1.0 / WIDTH)
    total = inv * (gain[...] * grad_norm) - x[...].astype(f32) * (inv * inv * mean)
    total = total + jnp.where(place[4] == 1, top[...].astype(f32), 0.0)
    own[...] = total
    low = total.astype(bf16)
    lower[...] = low[:64]
    upper[...] = low[64:]


def input_terms(place, gk, gv, wk, wv, x, top, gain, inverse, row):
    whole = lambda dims: pl.BlockSpec(dims, lambda i, p: (0, 0))
    tile = lambda rows: pl.BlockSpec((rows, 1024), lambda i, p: (0, i))
    weight = pl.BlockSpec((1024, COLS), lambda i, p: (i, 0))
    return pl.pallas_call(
        input_body,
        grid_spec=pltpu.PrefetchScalarGridSpec(
            num_scalar_prefetch=1,
            grid=(4,),
            in_specs=[
                whole((ROWS, COLS)),
                whole((ROWS, COLS)),
                weight,
                weight,
                tile(ROWS),
                tile(ROWS),
                tile(1),
                whole((ROWS, 128)),
                whole((ROWS, 128)),
            ],
            out_specs=[tile(ROWS), tile(64), tile(192)],
        ),
        out_shape=[shape((ROWS, WIDTH), f32), shape((64, WIDTH), bf16), shape((192, WIDTH), bf16)],
        cost_estimate=pl.CostEstimate(flops=2 * ROWS * WIDTH * 1024, bytes_accessed=18 << 20, transcendentals=0),
        name="input_terms",
        compiler_params=budget(24),
    )(place, gk, gv, wk, wv, x, top, gain, inverse, row)


def finish_body(own, lower, upper, out):
    part = pl.program_id(0)

    @pl.when(part == 0)
    def _():
        out[...] = (lower[...].astype(f32) + own[...]).astype(bf16)

    @pl.when(part != 0)
    def _():
        out[...] = (upper[...].astype(f32) + own[...]).astype(bf16)


def finish(own, lower, upper):
    return pl.pallas_call(
        finish_body,
        grid=(4,),
        in_specs=[
            pl.BlockSpec((64, WIDTH), lambda h: (h, 0)),
            pl.BlockSpec((64, WIDTH), lambda h: (0, 0)),
            pl.BlockSpec((64, WIDTH), lambda h: (jnp.maximum(h - 1, 0), 0)),
        ],
        out_specs=pl.BlockSpec((64, WIDTH), lambda h: (h, 0)),
        out_shape=shape((ROWS, WIDTH), bf16),
        cost_estimate=pl.CostEstimate(flops=ROWS * WIDTH, bytes_accessed=8 << 20, transcendentals=0),
        name="finish",
        compiler_params=budget(12),
    )(own, lower, upper)


def sum_body(place, own, r1, r3, out, *sends, axis):
    for k in (1, 3, 2, 0):
        rows = pl.ds(pl.multiple_of(((place[axis] + k) % 4) * 128, 128), 128)
        part = own[rows, :] + r1[rows, :].astype(f32) + r3[rows, :].astype(f32)
        if k == 0:
            out[...] = part
        else:
            sends[k - 1][...] = part.astype(bf16)


def sum_parts(place, own, r1, r3, axis):
    return pl.pallas_call(
        lambda *refs: sum_body(*refs, axis=axis),
        in_specs=[smem()] + [vmem()] * 3,
        out_specs=[vmem()] * 4,
        out_shape=[held((128, COLS), f32)] + [held((128, COLS), bf16)] * 3,
        name="sum_parts",
        compiler_params=budget(4),
    )(place, *hold(own, r1, r3))


def total_body(own, r1, r2, r3, out):
    part = own[...] + r1[...].astype(f32) + r2[...].astype(f32)
    out[...] = (part + r3[...].astype(f32)).astype(bf16)


def total(own, received):
    return pl.pallas_call(
        total_body,
        in_specs=[vmem()] * 4,
        out_specs=vmem(),
        out_shape=held((128, COLS), bf16),
        name="total",
        compiler_params=budget(4),
    )(*hold(own, *received))


def mean_body(own, other, out):
    out[...] = ((own[...].astype(f32) + other[...].astype(f32)) / REPLICAS).astype(bf16)


def mean(own, other):
    return pl.pallas_call(
        mean_body,
        in_specs=[vmem()] * 2,
        out_specs=vmem(),
        out_shape=held((128, COLS), bf16),
        name="mean",
        compiler_params=budget(4),
    )(*hold(own, other))


def stack_body(place, own, r1, r2, r3, out, *, axis):
    for k, ref in enumerate((own, r1, r2, r3)):
        rows = pl.ds(pl.multiple_of(((place[axis] - k + 4) % 4) * 128, 128), 128)
        out[rows, :] = ref[...]


def stack(place, own, received, axis):
    return pl.pallas_call(
        lambda *refs: stack_body(*refs, axis=axis),
        in_specs=[smem()] + [vmem()] * 4,
        out_specs=vmem(),
        out_shape=held((512, COLS), bf16),
        name="stack",
        compiler_params=budget(4),
    )(place, *hold(own, *received))


def assemble(place, entries, start=None):
    count = len(entries)
    extra = 0 if start is None else 2

    def body(*refs):
        place = refs[0]
        pieces = refs[1 : 1 + count]
        outs = refs[1 + count + extra : 3 + count + extra]
        sems = refs[3 + count + extra]
        copies = []
        for i, (which, k, swapped, first, piece) in enumerate(entries):
            core = (1 - place[3]) if swapped else place[3]
            member = (place[which] - k + 4) % 4
            rows = pl.ds(pl.multiple_of(core * 2048 + member * 512 + first, 256), piece.shape[0])
            copies.append(pltpu.make_async_copy(pieces[i], outs[which].at[rows, :], sems.at[i]))
        for copy in copies:
            copy.start()
        for copy in copies:
            copy.wait()

    anywhere = pl.BlockSpec(memory_space=pl.ANY)
    return pl.pallas_call(
        body,
        in_specs=[smem()] + [vmem()] * count + [anywhere] * extra,
        out_specs=[anywhere] * 2,
        out_shape=[shape((WIDTH, COLS), bf16)] * 2,
        scratch_shapes=[pltpu.SemaphoreType.DMA((count,))],
        input_output_aliases={} if start is None else {1 + count: 0, 2 + count: 1},
        name="assemble",
        compiler_params=budget(4),
    )(place, *hold(*[e[4] for e in entries]), *(() if start is None else start))


def ring(value, axis, steps):
    count = lax.axis_size(axis)
    return lax.ppermute(value, axis, [(i, (i + steps) % count) for i in range(count)])


def down(value):
    return lax.ppermute(value, "s", [(1, 0)])


def send_all(sends, axis):
    got = [None] * 3
    for k in (1, 3, 2):
        got[k - 1] = ring(sends[k - 1], axis, k)
    return got


X, Z = 0, 1


def all_steps(layer_inputs, norm_gain, queries, output_gradient, w_key, value_matrix, top_grad):
    place = jnp.stack([lax.axis_index(a).astype(jnp.int32) for a in ("x", "z", "y", "c", "s")])
    x, wk, wv = layer_inputs[0], w_key[0], value_matrix[0]
    send, mine, keys, values, inverse = project(place, x, norm_gain, wk, wv)
    theirs = ring(send, "c", 1)
    gk, gv, row = attend(queries[0], output_gradient[0], keys, values)
    gv_theirs = ring(gv, "c", 1)
    gk_theirs = ring(gk, "c", 1)
    chains = (
        ("k", (mine, theirs, gk, gk_theirs), Z, X, "z", "x"),
        ("v", (mine, theirs, gv, gv_theirs), X, Z, "x", "z"),
    )
    halves, near, gathered = {}, {}, {}
    for t, operands, first_at, second_at, first, second in chains:
        top, bottom = weight_far(place, *operands, first_at)
        halves[t] = (ring(top, first, 1), ring(bottom, first, 3))
    for t, operands, first_at, second_at, first, second in chains:
        kept, ahead, behind = weight_near(place, *operands, first_at)
        to_ahead, to_behind = relay(ahead, behind, *halves[t])
        near[t] = (kept, ring(to_ahead, first, 1), ring(to_behind, first, 3))
    own, lower, upper = input_terms(place, gk, gv, wk, wv, x, top_grad, norm_gain, inverse, row)
    lower_got = down(lower)
    for t, operands, first_at, second_at, first, second in chains:
        kept, *sends = sum_parts(place, *near[t], second_at)
        got = send_all(sends, second)
        part = total(kept, got)
        block = mean(part, ring(part, "y", 1))
        got = send_all([block] * 3, second)
        piece = stack(place, block, got, second_at)
        behind = ring(piece, first, 1)
        ahead = ring(piece, first, 3)
        top = ring(behind[:256], first, 1)
        bottom = ring(ahead[256:], first, 3)
        which = 1 if t == "k" else 0
        gathered[t] = [
            (which, 0, 0, piece),
            (which, 1, 0, behind),
            (which, 3, 0, ahead),
            (which, 2, 0, top),
            (which, 2, 256, bottom),
        ]
    entries = []
    for at in range(5):
        group = []
        for t in "vk":
            which, k, first_row, block = gathered[t][at]
            group.append((which, k, 0, first_row, block))
            group.append((which, k, 1, first_row, ring(block, "c", 1)))
        entries.append(group)
    upper_got = down(upper)
    part = assemble(place, entries[0])
    part = assemble(place, entries[1] + entries[2], part)
    value_grad, key_grad = assemble(place, entries[3] + entries[4], part)
    input_grad = finish(own, lower_got, upper_got)
    return (key_grad[None], value_grad[None], input_grad[None])


def solution(mesh):
    wide = Mesh(mesh.devices.reshape(2, 4, 4, 2, 2), ("s", "z", "x", "y", "c"))
    dp = ("z", "x", "y", "c")
    in_specs = (
        P("s", dp, None),
        P("s", None),
        P("s", dp, None),
        P("s", dp, None),
        P("s", None, None),
        P("s", None, None),
        P(dp, None),
    )
    out_specs = (P("s", None, None), P("s", None, None), P("s", dp, None))
    return jax.shard_map(all_steps, mesh=wide, in_specs=in_specs, out_specs=out_specs, check_vma=False)
```

time: 182 us -> 159 us (0.87)
  waiting for transfers between devices: 85.9 us -> 68.6 us
  local copies, waits for them, and re-layouts: 6.78 us -> 0.91 us
    ppermute x37 -> x43, waiting for transfers between devices: 85.9 us -> 68.6 us  [ring(): lax.ppermute(value, axis, [(i, (i + steps) % count) for i in range(count)])]
    unnamed x14 -> x16, local copies, waits for them, and re-layouts: 6.7 us -> 0.75 us
    pallas_call x1, Pallas kernels: 6.32 us -> 8.21 us  [project(): pl.pallas_call(project_body, grid_spec=pltpu.PrefetchScalarGridSpec(num_s...]
    ppermute x37 -> x43, starting transfers between devices: 47.5 us -> 48.8 us  [ring(): lax.ppermute(value, axis, [(i, (i + steps) % count) for i in range(count)])]
    pallas_call x2 -> x3, Pallas kernels: 5.24 us -> 6.45 us  [assemble(): pl.pallas_call(body, in_specs=[smem()] + [vmem()] * count + [anywhere] *...]
    pallas_call x5 -> x11, Pallas kernels: 8.34 us -> 7.74 us  [the longest x2 3.15 us: weight_near(): pl.pallas_call(lambda *refs: weight_near_body(*refs, axis=axis), in_specs...]
  transfers between devices with their start and end apart: 39 -> 45, of which waited for: 15 -> 15; matrix products, arithmetic and copies ran while one was open for 0% -> 0% of each run, Pallas kernels for 13% -> 15%
where the time goes in v2:
time: 159 us
  waiting for transfers between devices  68.6 us (43%)
  starting transfers between devices  52.4 us (33%)
  Pallas kernels  35.5 us (22%)
    ppermute x43, waiting for transfers between devices, ring(): lax.ppermute(value, axis, [(i, (i + steps) % count) for i in range(count)])  68.6 us
    ppermute x43, starting transfers between devices, ring(): lax.ppermute(value, axis, [(i, (i + steps) % count) for i in range(count)])  48.8 us
    pallas_call x1, Pallas kernels, project(): pl.pallas_call(project_body, grid_spec=pltpu.PrefetchScalarGridSpec(num_s...  8.21 us
    pallas_call x3, Pallas kernels, assemble(): pl.pallas_call(body, in_specs=[smem()] + [vmem()] * count + [anywhere] *...  6.45 us
    pallas_call x1, Pallas kernels, attend(): pl.pallas_call(attend_body, grid=(2, 4), in_specs=[wide, wide, head, head...  5.71 us
    pallas_call x1, Pallas kernels, input_terms(): pl.pallas_call(input_body, grid_spec=pltpu.PrefetchScalarGridSpec(num_sca...  4.81 us
    ppermute x2, starting transfers between devices, down(): return lax.ppermute(value, 's', [(1, 0)])  3.66 us
  transfers between devices with their start and end apart: 45, of which 15 were waited for; matrix products, arithmetic and copies ran while one was open for 0% of the time, Pallas kernels for 15%

profile of v2, /device:TPU:16, one launch (start us, length us, event | category | flops | bytes accessed | tf_op | source)
XLA Modules:
  0.0 158.7 jit_solution(6297084607995577730)
XLA Ops:
  1.4 8.2 %project.1 = (bf16[256,2048]{1,0:T(8,128)(2,1)S(1)}, bf16[256,2048]{1,0:T(8,128)(2,1)S(1)}, f32[256,512]{1,0:T(8,128)S(1)}, f32[256,512]{1,0:T(8,128)S(1)}, f32[256,128]{1,0:T(8,128)S(1)}) custom-call(s32[5]{0:T(128)S(1)} %stack.25.place.refs_0_, bf16[256,4096]{1,0:T(8,128)(2,1)} %bitcast.17, f32[1,4096]{1,0:T(1,128)S(1)} %copy-done.4, ...), custom_call_target="tpu_custom_call" | custom-call | flops 2147483648 | bytes 12582912 | tf_op jit(solution)/shard_map/project/pallas_call | solution.py:88
  9.8 5.7 %attend.1 = (bf16[256,512]{1,0:T(8,128)(2,1)S(1)}, bf16[256,512]{1,0:T(8,128)(2,1)S(1)}, f32[256,128]{1,0:T(8,128)S(1)}) custom-call(bf16[256,2048]{1,0:T(8,128)(2,1)S(1)} %bitcast.19, bf16[256,2048]{1,0:T(8,128)(2,1)S(1)} %bitcast.20, f32[256,512]{1,0:T(8,128)S(1)} %get-tuple-element.44.kf, f32[256,512]{1,0:T(8,128)S(1)} %get-tuple-element.45.vf), custom_call_target="tpu_custom_call" | custom-call | flops 2400000000 | bytes 4194304 | tf_op jit(solution)/shard_map/attend/pallas_call | solution.py:161
  18.2 2.0 %collective-permute-start.17 = (bf16[256,512]{1,0:T(8,128)(2,1)S(1)}, bf16[256,512]{1,0:T(8,128)(2,1)S(1)}, u32[]{:S(2)}, u32[]{:S(2)}) collective-permute-start(bf16[256,512]{1,0:T(8,128)(2,1)S(1)} %get-tuple-element.62), channel_id=1, source_target_pairs={{0,16},{16,32},{32,48},{48,0},{1,17},{17,33},{33,49},{49,1},{2,18}... | collective-permute-start | bytes 786440 | tf_op jit(solution)/shard_map/ppermute | solution.py:411
  20.2 2.2 %collective-permute-start.18 = (bf16[256,512]{1,0:T(8,128)(2,1)S(1)}, bf16[256,512]{1,0:T(8,128)(2,1)S(1)}, u32[]{:S(2)}, u32[]{:S(2)}) collective-permute-start(bf16[256,512]{1,0:T(8,128)(2,1)S(1)} %get-tuple-element.63), channel_id=1, source_target_pairs={{0,48},{16,0},{32,16},{48,32},{1,49},{17,1},{33,17},{49,33},{2,50}... | collective-permute-start | bytes 786440 | tf_op jit(solution)/shard_map/ppermute | solution.py:411
  24.1 5.1 %collective-permute-done.17.top = bf16[256,512]{1,0:T(8,128)(2,1)S(1)} collective-permute-done((bf16[256,512]{1,0:T(8,128)(2,1)S(1)}, bf16[256,512]{1,0:T(8,128)(2,1)S(1)}, u32[]{:S(2)}, u32[]{:S(2)}) %collective-permute-start.17) | collective-permute-done | bytes 262176 | tf_op jit(solution)/shard_map/ppermute | solution.py:411
  30.7 2.0 %collective-permute-start.20 = (bf16[512,512]{1,0:T(8,128)(2,1)S(1)}, bf16[512,512]{1,0:T(8,128)(2,1)S(1)}, u32[]{:S(2)}, u32[]{:S(2)}) collective-permute-start(bf16[512,512]{1,0:T(8,128)(2,1)S(1)} %get-tuple-element.65), channel_id=1, source_target_pairs={{0,48},{16,0},{32,16},{48,32},{1,49},{17,1},{33,17},{49,33},{2,50}... | collective-permute-start | bytes 1572872 | tf_op jit(solution)/shard_map/ppermute | solution.py:411
  38.6 3.9 %collective-permute-done.2.top = bf16[256,512]{1,0:T(8,128)(2,1)S(1)} collective-permute-done((bf16[256,512]{1,0:T(8,128)(2,1)S(1)}, bf16[256,512]{1,0:T(8,128)(2,1)S(1)}, u32[]{:S(2)}, u32[]{:S(2)}) %collective-permute-start.2) | collective-permute-done | bytes 262176 | tf_op jit(solution)/shard_map/ppermute | solution.py:411
  47.0 2.9 %collective-permute-start.22 = (bf16[128,512]{1,0:T(8,128)(2,1)S(1)}, bf16[128,512]{1,0:T(8,128)(2,1)S(1)}, u32[]{:S(2)}, u32[]{:S(2)}) collective-permute-start(bf16[128,512]{1,0:T(8,128)(2,1)S(1)} %get-tuple-element.68), channel_id=1, source_target_pairs={{0,8},{4,12},{8,0},{12,4},{1,9},{5,13},{9,1},{13,5},{2,10},{6,14},... | collective-permute-start | bytes 393224 | tf_op jit(solution)/shard_map/ppermute | solution.py:411
  49.9 4.8 %input_terms.1 = (f32[256,4096]{1,0:T(8,128)S(1)}, bf16[64,4096]{1,0:T(8,128)(2,1)S(1)}, bf16[192,4096]{1,0:T(8,128)(2,1)S(1)}) custom-call(s32[5]{0:T(128)S(1)} %stack.25.place.refs_0_, bf16[256,512]{1,0:T(8,128)(2,1)S(1)} %get-tuple-element.58.refs_3_.gk, bf16[256,512]{1,0:T(8,128)(2,1)S(1)} %get-tuple-element.46.refs_3_.gv, ...), custom_call_target="tpu_custom_call" | custom-call | flops 2147483648 | bytes 18874368 | tf_op jit(solution)/shard_map/input_terms/pallas_call | solution.py:253
  54.7 2.3 %collective-permute-start.44 = (bf16[192,4096]{1,0:T(8,128)(2,1)S(1)}, bf16[192,4096]{1,0:T(8,128)(2,1)S(1)}, u32[]{:S(2)}, u32[]{:S(2)}) collective-permute-start(bf16[192,4096]{1,0:T(8,128)(2,1)S(1)} %get-tuple-element.80), channel_id=1, source_target_pairs={{64,0},{65,1},{66,2},{67,3},{68,4},{69,5},{70,6},{71,7},{72,8},{73... | collective-permute-start | bytes 4718600 | tf_op jit(solution)/shard_map/ppermute | solution.py:415
  58.0 2.3 %collective-permute-start.23 = (bf16[128,512]{1,0:T(8,128)(2,1)S(1)}, bf16[128,512]{1,0:T(8,128)(2,1)S(1)}, u32[]{:S(2)}, u32[]{:S(2)}) collective-permute-start(bf16[128,512]{1,0:T(8,128)(2,1)S(1)} %get-tuple-element.69), channel_id=1, source_target_pairs={{0,12},{4,0},{8,4},{12,8},{1,13},{5,1},{9,5},{13,9},{2,14},{6,2},{... | collective-permute-start | bytes 393224 | tf_op jit(solution)/shard_map/ppermute | solution.py:411
  61.2 2.7 %collective-permute-start.7 = (bf16[128,512]{1,0:T(8,128)(2,1)S(1)}, bf16[128,512]{1,0:T(8,128)(2,1)S(1)}, u32[]{:S(2)}, u32[]{:S(2)}) collective-permute-start(bf16[128,512]{1,0:T(8,128)(2,1)S(1)} %get-tuple-element.56), channel_id=1, source_target_pairs={{0,32},{16,48},{32,0},{48,16},{1,33},{17,49},{33,1},{49,17},{2,34}... | collective-permute-start | bytes 393224 | tf_op jit(solution)/shard_map/ppermute | solution.py:411
  64.7 2.0 %collective-permute-start.24 = (bf16[128,512]{1,0:T(8,128)(2,1)S(1)}, bf16[128,512]{1,0:T(8,128)(2,1)S(1)}, u32[]{:S(2)}, u32[]{:S(2)}) collective-permute-start(bf16[128,512]{1,0:T(8,128)(2,1)S(1)} %total.3.own), channel_id=1, source_target_pairs={{0,2},{2,0},{1,3},{3,1},{4,6},{6,4},{5,7},{7,5},{8,10},{10,8},{9,1... | collective-permute-start | bytes 393224 | tf_op jit(solution)/shard_map/ppermute | solution.py:411
  66.6 2.1 %collective-permute-done.6.r1 = bf16[128,512]{1,0:T(8,128)(2,1)S(1)} collective-permute-done((bf16[128,512]{1,0:T(8,128)(2,1)S(1)}, bf16[128,512]{1,0:T(8,128)(2,1)S(1)}, u32[]{:S(2)}, u32[]{:S(2)}) %collective-permute-start.6) | collective-permute-done | bytes 131104 | tf_op jit(solution)/shard_map/ppermute | solution.py:411
  71.0 24.4 %collective-permute-done.24.other = bf16[128,512]{1,0:T(8,128)(2,1)S(1)} collective-permute-done((bf16[128,512]{1,0:T(8,128)(2,1)S(1)}, bf16[128,512]{1,0:T(8,128)(2,1)S(1)}, u32[]{:S(2)}, u32[]{:S(2)}) %collective-permute-start.24) | collective-permute-done | bytes 131104 | tf_op jit(solution)/shard_map/ppermute | solution.py:411
  95.9 2.5 %collective-permute-start.26 = (bf16[128,512]{1,0:T(8,128)(2,1)S(1)}, bf16[128,512]{1,0:T(8,128)(2,1)S(1)}, u32[]{:S(2)}, u32[]{:S(2)}) collective-permute-start(bf16[128,512]{1,0:T(8,128)(2,1)S(1)} %mean.3.refs_1_), channel_id=1, source_target_pairs={{0,8},{4,12},{8,0},{12,4},{1,9},{5,13},{9,1},{13,5},{2,10},{6,14},... | collective-permute-start | bytes 393224 | tf_op jit(solution)/shard_map/ppermute | solution.py:411
  99.3 3.8 %collective-permute-done.25.refs_2_ = bf16[128,512]{1,0:T(8,128)(2,1)S(1)} collective-permute-done((bf16[128,512]{1,0:T(8,128)(2,1)S(1)}, bf16[128,512]{1,0:T(8,128)(2,1)S(1)}, u32[]{:S(2)}, u32[]{:S(2)}) %collective-permute-start.25) | collective-permute-done | bytes 131104 | tf_op jit(solution)/shard_map/ppermute | solution.py:411
  104.4 2.2 %collective-permute-start.11 = (bf16[128,512]{1,0:T(8,128)(2,1)S(1)}, bf16[128,512]{1,0:T(8,128)(2,1)S(1)}, u32[]{:S(2)}, u32[]{:S(2)}) collective-permute-start(bf16[128,512]{1,0:T(8,128)(2,1)S(1)} %mean.2.refs_1_), channel_id=1, source_target_pairs={{0,32},{16,48},{32,0},{48,16},{1,33},{17,49},{33,1},{49,17},{2,34}... | collective-permute-start | bytes 393224 | tf_op jit(solution)/shard_map/ppermute | solution.py:411
  108.7 1.9 %collective-permute-start.34 = (bf16[512,512]{1,0:T(8,128)(2,1)S(1)}, bf16[512,512]{1,0:T(8,128)(2,1)S(1)}, u32[]{:S(2)}, u32[]{:S(2)}) collective-permute-start(bf16[512,512]{1,0:T(8,128)(2,1)S(1)} %stack.27.refs_3_), channel_id=1, source_target_pairs={{0,48},{16,0},{32,16},{48,32},{1,49},{17,1},{33,17},{49,33},{2,50}... | collective-permute-start | bytes 1572872 | tf_op jit(solution)/shard_map/ppermute | solution.py:411
  110.6 1.8 %collective-permute-done.11.refs_3_ = bf16[128,512]{1,0:T(8,128)(2,1)S(1)} collective-permute-done((bf16[128,512]{1,0:T(8,128)(2,1)S(1)}, bf16[128,512]{1,0:T(8,128)(2,1)S(1)}, u32[]{:S(2)}, u32[]{:S(2)}) %collective-permute-start.11) | collective-permute-done | bytes 131104 | tf_op jit(solution)/shard_map/ppermute | solution.py:411
  112.4 2.7 %collective-permute-start.12 = (bf16[128,512]{1,0:T(8,128)(2,1)S(1)}, bf16[128,512]{1,0:T(8,128)(2,1)S(1)}, u32[]{:S(2)}, u32[]{:S(2)}) collective-permute-start(bf16[128,512]{1,0:T(8,128)(2,1)S(1)} %mean.2.refs_1_), channel_id=1, source_target_pairs={{0,48},{16,0},{32,16},{48,32},{1,49},{17,1},{33,17},{49,33},{2,50}... | collective-permute-start | bytes 393224 | tf_op jit(solution)/shard_map/ppermute | solution.py:411
  115.1 5.5 %collective-permute-done.12.refs_4_ = bf16[128,512]{1,0:T(8,128)(2,1)S(1)} collective-permute-done((bf16[128,512]{1,0:T(8,128)(2,1)S(1)}, bf16[128,512]{1,0:T(8,128)(2,1)S(1)}, u32[]{:S(2)}, u32[]{:S(2)}) %collective-permute-start.12) | collective-permute-done | bytes 131104 | tf_op jit(solution)/shard_map/ppermute | solution.py:411
  121.9 3.1 %collective-permute-start.31 = (bf16[512,512]{1,0:T(8,128)(2,1)S(1)}, bf16[512,512]{1,0:T(8,128)(2,1)S(1)}, u32[]{:S(2)}, u32[]{:S(2)}) collective-permute-start(bf16[512,512]{1,0:T(8,128)(2,1)S(1)} %stack.26.refs_1_), channel_id=1, source_target_pairs={{0,12},{4,0},{8,4},{12,8},{1,13},{5,1},{9,5},{13,9},{2,14},{6,2},{... | collective-permute-start | bytes 1572872 | tf_op jit(solution)/shard_map/ppermute | solution.py:411
  125.0 6.7 %collective-permute-done.13.refs_1_ = bf16[512,512]{1,0:T(8,128)(2,1)S(1)} collective-permute-done((bf16[512,512]{1,0:T(8,128)(2,1)S(1)}, bf16[512,512]{1,0:T(8,128)(2,1)S(1)}, u32[]{:S(2)}, u32[]{:S(2)}) %collective-permute-start.13) | collective-permute-done | bytes 524320 | tf_op jit(solution)/shard_map/ppermute | solution.py:411
  133.3 2.6 %collective-permute-start.35 = (bf16[256,512]{1,0:T(8,128)(2,1)S(1)}, bf16[256,512]{1,0:T(8,128)(2,1)S(1)}, u32[]{:S(2)}, u32[]{:S(2)}) collective-permute-start(bf16[256,512]{1,0:T(8,128)(2,1)S(1)} %slice.19), channel_id=1, source_target_pairs={{0,48},{16,0},{32,16},{48,32},{1,49},{17,1},{33,17},{49,33},{2,50}... | collective-permute-start | bytes 786440 | tf_op jit(solution)/shard_map/ppermute | solution.py:411
  136.5 3.6 %collective-permute-done.29.refs_3_ = bf16[256,512]{1,0:T(8,128)(2,1)S(1)} collective-permute-done((bf16[256,512]{1,0:T(8,128)(2,1)S(1)}, bf16[256,512]{1,0:T(8,128)(2,1)S(1)}, u32[]{:S(2)}, u32[]{:S(2)}) %collective-permute-start.29) | collective-permute-done | bytes 262176 | tf_op jit(solution)/shard_map/ppermute | solution.py:411
  140.8 2.7 %collective-permute-done.14.refs_1_ = bf16[256,512]{1,0:T(8,128)(2,1)S(1)} collective-permute-done((bf16[256,512]{1,0:T(8,128)(2,1)S(1)}, bf16[256,512]{1,0:T(8,128)(2,1)S(1)}, u32[]{:S(2)}, u32[]{:S(2)}) %collective-permute-start.14) | collective-permute-done | bytes 262176 | tf_op jit(solution)/shard_map/ppermute | solution.py:411
  143.5 5.5 %collective-permute-done.32.refs_5_ = bf16[256,512]{1,0:T(8,128)(2,1)S(1)} collective-permute-done((bf16[256,512]{1,0:T(8,128)(2,1)S(1)}, bf16[256,512]{1,0:T(8,128)(2,1)S(1)}, u32[]{:S(2)}, u32[]{:S(2)}) %collective-permute-start.32) | collective-permute-done | bytes 262176 | tf_op jit(solution)/shard_map/ppermute | solution.py:411
  150.0 2.0 %finish.1 = bf16[256,4096]{1,0:T(8,128)(2,1)} custom-call(f32[256,4096]{1,0:T(8,128)S(1)} %get-tuple-element.78.own, bf16[64,4096]{1,0:T(8,128)(2,1)S(1)} %collective-permute-done.43.lower, bf16[192,4096]{1,0:T(8,128)(2,1)S(1)} %collective-permute-done.44.upper), custom_call_target="tpu_custom_call" | custom-call | flops 1048576 | bytes 8388608 | tf_op jit(solution)/shard_map/finish/pallas_call | solution.py:291
  152.0 1.9 %assemble.3 = (bf16[4096,512]{1,0:T(8,128)(2,1)}, bf16[4096,512]{1,0:T(8,128)(2,1)}) custom-call(s32[5]{0:T(128)S(1)} %stack.25.place.refs_0_, bf16[512,512]{1,0:T(8,128)(2,1)S(1)} %stack.26.refs_1_, bf16[512,512]{1,0:T(8,128)(2,1)S(1)} %collective-permute-done.41.refs_2_, bf16[512,512]{1,0:T(8,128)(2,1)S(1)} %stack.27.refs_3_, ...), custom_call_target="tpu_custom_call" | custom-call | tf_op jit(solution)/shard_map/assemble/pallas_call | solution.py:397
  153.9 2.6 %assemble.4 = (bf16[4096,512]{1,0:T(8,128)(2,1)}, bf16[4096,512]{1,0:T(8,128)(2,1)}) custom-call(s32[5]{0:T(128)S(1)} %stack.25.place.refs_0_, bf16[512,512]{1,0:T(8,128)(2,1)S(1)} %collective-permute-done.13.refs_1_, bf16[512,512]{1,0:T(8,128)(2,1)S(1)} %collective-permute-done.37.refs_2_, ...), custom_call_target="tpu_custom_call", output_to_operand_aliasing={{0}: (9, {}), {1}: (10, {})} | custom-call | tf_op jit(solution)/shard_map/assemble/pallas_call | solution.py:397
  156.6 1.9 %assemble.5 = (bf16[4096,512]{1,0:T(8,128)(2,1)}, bf16[4096,512]{1,0:T(8,128)(2,1)}) custom-call(s32[5]{0:T(128)S(1)} %stack.25.place.refs_0_, bf16[256,512]{1,0:T(8,128)(2,1)S(1)} %collective-permute-done.14.refs_1_, bf16[256,512]{1,0:T(8,128)(2,1)S(1)} %collective-permute-done.15.refs_2_, ...), custom_call_target="tpu_custom_call", output_to_operand_aliasing={{0}: (9, {}), {1}: (10, {})} | custom-call | tf_op jit(solution)/shard_map/assemble/pallas_call | solution.py:397
  (100 shorter events, 31.8 us)
Async XLA Ops:
  18.2 10.9 %collective-permute-start.17 = (bf16[256,512]{1,0:T(8,128)(2,1)S(1)}, bf16[256,512]{1,0:T(8,128)(2,1)S(1)}, u32[]{:S(2)}, u32[]{:S(2)}) collective-permute-start(bf16[256,512]{1,0:T(8,128)(2,1)S(1)} %get-tuple-element.62), channel_id=1, source_target_pairs={{0,16},{16,32},{32,48},{48,0},{1,17},{17,33},{33,49},{49,1},{2,18}... | collective-permute-start | bytes 786440 | tf_op jit(solution)/shard_map/ppermute | solution.py:411
  20.2 8.9 %collective-permute-start.18 = (bf16[256,512]{1,0:T(8,128)(2,1)S(1)}, bf16[256,512]{1,0:T(8,128)(2,1)S(1)}, u32[]{:S(2)}, u32[]{:S(2)}) collective-permute-start(bf16[256,512]{1,0:T(8,128)(2,1)S(1)} %get-tuple-element.63), channel_id=1, source_target_pairs={{0,48},{16,0},{32,16},{48,32},{1,49},{17,1},{33,17},{49,33},{2,50}... | collective-permute-start | bytes 786440 | tf_op jit(solution)/shard_map/ppermute | solution.py:411
  22.4 10.3 %collective-permute-start.1 = (bf16[256,512]{1,0:T(8,128)(2,1)S(1)}, bf16[256,512]{1,0:T(8,128)(2,1)S(1)}, u32[]{:S(2)}, u32[]{:S(2)}) collective-permute-start(bf16[256,512]{1,0:T(8,128)(2,1)S(1)} %get-tuple-element.46.refs_3_.gv), channel_id=1, source_target_pairs={{0,1},{1,0},{2,3},{3,2},{4,5},{5,4},{6,7},{7,6},{8,9},{9,8},{10,11... | collective-permute-start | bytes 786440 | tf_op jit(solution)/shard_map/ppermute | solution.py:411
  29.3 16.6 %collective-permute-start.19 = (bf16[512,512]{1,0:T(8,128)(2,1)S(1)}, bf16[512,512]{1,0:T(8,128)(2,1)S(1)}, u32[]{:S(2)}, u32[]{:S(2)}) collective-permute-start(bf16[512,512]{1,0:T(8,128)(2,1)S(1)} %get-tuple-element.64), channel_id=1, source_target_pairs={{0,16},{16,32},{32,48},{48,0},{1,17},{17,33},{33,49},{49,1},{2,18}... | collective-permute-start | bytes 1572872 | tf_op jit(solution)/shard_map/ppermute | solution.py:411
  30.7 15.2 %collective-permute-start.20 = (bf16[512,512]{1,0:T(8,128)(2,1)S(1)}, bf16[512,512]{1,0:T(8,128)(2,1)S(1)}, u32[]{:S(2)}, u32[]{:S(2)}) collective-permute-start(bf16[512,512]{1,0:T(8,128)(2,1)S(1)} %get-tuple-element.65), channel_id=1, source_target_pairs={{0,48},{16,0},{32,16},{48,32},{1,49},{17,1},{33,17},{49,33},{2,50}... | collective-permute-start | bytes 1572872 | tf_op jit(solution)/shard_map/ppermute | solution.py:411
  33.7 8.7 %collective-permute-start.2 = (bf16[256,512]{1,0:T(8,128)(2,1)S(1)}, bf16[256,512]{1,0:T(8,128)(2,1)S(1)}, u32[]{:S(2)}, u32[]{:S(2)}) collective-permute-start(bf16[256,512]{1,0:T(8,128)(2,1)S(1)} %get-tuple-element.50), channel_id=1, source_target_pairs={{0,4},{4,8},{8,12},{12,0},{1,5},{5,9},{9,13},{13,1},{2,6},{6,10},{... | collective-permute-start | bytes 786440 | tf_op jit(solution)/shard_map/ppermute | solution.py:411
  42.6 15.4 %collective-permute-start.4 = (bf16[512,512]{1,0:T(8,128)(2,1)S(1)}, bf16[512,512]{1,0:T(8,128)(2,1)S(1)}, u32[]{:S(2)}, u32[]{:S(2)}) collective-permute-start(bf16[512,512]{1,0:T(8,128)(2,1)S(1)} %get-tuple-element.52), channel_id=1, source_target_pairs={{0,4},{4,8},{8,12},{12,0},{1,5},{5,9},{9,13},{13,1},{2,6},{6,10},{... | collective-permute-start | bytes 1572872 | tf_op jit(solution)/shard_map/ppermute | solution.py:411
  44.1 16.2 %collective-permute-start.5 = (bf16[512,512]{1,0:T(8,128)(2,1)S(1)}, bf16[512,512]{1,0:T(8,128)(2,1)S(1)}, u32[]{:S(2)}, u32[]{:S(2)}) collective-permute-start(bf16[512,512]{1,0:T(8,128)(2,1)S(1)} %get-tuple-element.53), channel_id=1, source_target_pairs={{0,12},{4,0},{8,4},{12,8},{1,13},{5,1},{9,5},{13,9},{2,14},{6,2},{... | collective-permute-start | bytes 1572872 | tf_op jit(solution)/shard_map/ppermute | solution.py:411
  46.6 14.5 %collective-permute-start.21 = (bf16[128,512]{1,0:T(8,128)(2,1)S(1)}, bf16[128,512]{1,0:T(8,128)(2,1)S(1)}, u32[]{:S(2)}, u32[]{:S(2)}) collective-permute-start(bf16[128,512]{1,0:T(8,128)(2,1)S(1)} %get-tuple-element.67), channel_id=1, source_target_pairs={{0,4},{4,8},{8,12},{12,0},{1,5},{5,9},{9,13},{13,1},{2,6},{6,10},{... | collective-permute-start | bytes 393224 | tf_op jit(solution)/shard_map/ppermute | solution.py:411
  47.0 16.9 %collective-permute-start.22 = (bf16[128,512]{1,0:T(8,128)(2,1)S(1)}, bf16[128,512]{1,0:T(8,128)(2,1)S(1)}, u32[]{:S(2)}, u32[]{:S(2)}) collective-permute-start(bf16[128,512]{1,0:T(8,128)(2,1)S(1)} %get-tuple-element.68), channel_id=1, source_target_pairs={{0,8},{4,12},{8,0},{12,4},{1,9},{5,13},{9,1},{13,5},{2,10},{6,14},... | collective-permute-start | bytes 393224 | tf_op jit(solution)/shard_map/ppermute | solution.py:411
  54.7 78.5 %collective-permute-start.44 = (bf16[192,4096]{1,0:T(8,128)(2,1)S(1)}, bf16[192,4096]{1,0:T(8,128)(2,1)S(1)}, u32[]{:S(2)}, u32[]{:S(2)}) collective-permute-start(bf16[192,4096]{1,0:T(8,128)(2,1)S(1)} %get-tuple-element.80), channel_id=1, source_target_pairs={{64,0},{65,1},{66,2},{67,3},{68,4},{69,5},{70,6},{71,7},{72,8},{73... | collective-permute-start | bytes 4718600 | tf_op jit(solution)/shard_map/ppermute | solution.py:415
  61.1 7.7 %collective-permute-start.6 = (bf16[128,512]{1,0:T(8,128)(2,1)S(1)}, bf16[128,512]{1,0:T(8,128)(2,1)S(1)}, u32[]{:S(2)}, u32[]{:S(2)}) collective-permute-start(bf16[128,512]{1,0:T(8,128)(2,1)S(1)} %get-tuple-element.55), channel_id=1, source_target_pairs={{0,16},{16,32},{32,48},{48,0},{1,17},{17,33},{33,49},{49,1},{2,18}... | collective-permute-start | bytes 393224 | tf_op jit(solution)/shard_map/ppermute | solution.py:411
  64.7 30.7 %collective-permute-start.24 = (bf16[128,512]{1,0:T(8,128)(2,1)S(1)}, bf16[128,512]{1,0:T(8,128)(2,1)S(1)}, u32[]{:S(2)}, u32[]{:S(2)}) collective-permute-start(bf16[128,512]{1,0:T(8,128)(2,1)S(1)} %total.3.own), channel_id=1, source_target_pairs={{0,2},{2,0},{1,3},{3,1},{4,6},{6,4},{5,7},{7,5},{8,10},{10,8},{9,1... | collective-permute-start | bytes 393224 | tf_op jit(solution)/shard_map/ppermute | solution.py:411
  69.7 29.3 %collective-permute-start.9 = (bf16[128,512]{1,0:T(8,128)(2,1)S(1)}, bf16[128,512]{1,0:T(8,128)(2,1)S(1)}, u32[]{:S(2)}, u32[]{:S(2)}) collective-permute-start(bf16[128,512]{1,0:T(8,128)(2,1)S(1)} %total.2.own), channel_id=1, source_target_pairs={{0,2},{2,0},{1,3},{3,1},{4,6},{6,4},{5,7},{7,5},{8,10},{10,8},{9,1... | collective-permute-start | bytes 393224 | tf_op jit(solution)/shard_map/ppermute | solution.py:411
  95.9 8.5 %collective-permute-start.26 = (bf16[128,512]{1,0:T(8,128)(2,1)S(1)}, bf16[128,512]{1,0:T(8,128)(2,1)S(1)}, u32[]{:S(2)}, u32[]{:S(2)}) collective-permute-start(bf16[128,512]{1,0:T(8,128)(2,1)S(1)} %mean.3.refs_1_), channel_id=1, source_target_pairs={{0,8},{4,12},{8,0},{12,4},{1,9},{5,13},{9,1},{13,5},{2,10},{6,14},... | collective-permute-start | bytes 393224 | tf_op jit(solution)/shard_map/ppermute | solution.py:411
  98.4 8.2 %collective-permute-start.27 = (bf16[128,512]{1,0:T(8,128)(2,1)S(1)}, bf16[128,512]{1,0:T(8,128)(2,1)S(1)}, u32[]{:S(2)}, u32[]{:S(2)}) collective-permute-start(bf16[128,512]{1,0:T(8,128)(2,1)S(1)} %mean.3.refs_1_), channel_id=1, source_target_pairs={{0,12},{4,0},{8,4},{12,8},{1,13},{5,1},{9,5},{13,9},{2,14},{6,2},{... | collective-permute-start | bytes 393224 | tf_op jit(solution)/shard_map/ppermute | solution.py:411
  99.0 9.7 %collective-permute-start.10 = (bf16[128,512]{1,0:T(8,128)(2,1)S(1)}, bf16[128,512]{1,0:T(8,128)(2,1)S(1)}, u32[]{:S(2)}, u32[]{:S(2)}) collective-permute-start(bf16[128,512]{1,0:T(8,128)(2,1)S(1)} %mean.2.refs_1_), channel_id=1, source_target_pairs={{0,16},{16,32},{32,48},{48,0},{1,17},{17,33},{33,49},{49,1},{2,18}... | collective-permute-start | bytes 393224 | tf_op jit(solution)/shard_map/ppermute | solution.py:411
  103.1 18.2 %collective-permute-start.43 = (bf16[64,4096]{1,0:T(8,128)(2,1)S(1)}, bf16[64,4096]{1,0:T(8,128)(2,1)S(1)}, u32[]{:S(2)}, u32[]{:S(2)}) collective-permute-start(bf16[64,4096]{1,0:T(8,128)(2,1)S(1)} %get-tuple-element.79), channel_id=1, source_target_pairs={{64,0},{65,1},{66,2},{67,3},{68,4},{69,5},{70,6},{71,7},{72,8},{73... | collective-permute-start | bytes 1572872 | tf_op jit(solution)/shard_map/ppermute | solution.py:415
  104.4 8.0 %collective-permute-start.11 = (bf16[128,512]{1,0:T(8,128)(2,1)S(1)}, bf16[128,512]{1,0:T(8,128)(2,1)S(1)}, u32[]{:S(2)}, u32[]{:S(2)}) collective-permute-start(bf16[128,512]{1,0:T(8,128)(2,1)S(1)} %mean.2.refs_1_), channel_id=1, source_target_pairs={{0,32},{16,48},{32,0},{48,16},{1,33},{17,49},{33,1},{49,17},{2,34}... | collective-permute-start | bytes 393224 | tf_op jit(solution)/shard_map/ppermute | solution.py:411
  107.3 14.1 %collective-permute-start.28 = (bf16[512,512]{1,0:T(8,128)(2,1)S(1)}, bf16[512,512]{1,0:T(8,128)(2,1)S(1)}, u32[]{:S(2)}, u32[]{:S(2)}) collective-permute-start(bf16[512,512]{1,0:T(8,128)(2,1)S(1)} %stack.27.refs_3_), channel_id=1, source_target_pairs={{0,16},{16,32},{32,48},{48,0},{1,17},{17,33},{33,49},{49,1},{2,18}... | collective-permute-start | bytes 1572872 | tf_op jit(solution)/shard_map/ppermute | solution.py:411
  108.7 13.2 %collective-permute-start.34 = (bf16[512,512]{1,0:T(8,128)(2,1)S(1)}, bf16[512,512]{1,0:T(8,128)(2,1)S(1)}, u32[]{:S(2)}, u32[]{:S(2)}) collective-permute-start(bf16[512,512]{1,0:T(8,128)(2,1)S(1)} %stack.27.refs_3_), channel_id=1, source_target_pairs={{0,48},{16,0},{32,16},{48,32},{1,49},{17,1},{33,17},{49,33},{2,50}... | collective-permute-start | bytes 1572872 | tf_op jit(solution)/shard_map/ppermute | solution.py:411
  112.4 8.2 %collective-permute-start.12 = (bf16[128,512]{1,0:T(8,128)(2,1)S(1)}, bf16[128,512]{1,0:T(8,128)(2,1)S(1)}, u32[]{:S(2)}, u32[]{:S(2)}) collective-permute-start(bf16[128,512]{1,0:T(8,128)(2,1)S(1)} %mean.2.refs_1_), channel_id=1, source_target_pairs={{0,48},{16,0},{32,16},{48,32},{1,49},{17,1},{33,17},{49,33},{2,50}... | collective-permute-start | bytes 393224 | tf_op jit(solution)/shard_map/ppermute | solution.py:411
  121.2 10.6 %collective-permute-start.13 = (bf16[512,512]{1,0:T(8,128)(2,1)S(1)}, bf16[512,512]{1,0:T(8,128)(2,1)S(1)}, u32[]{:S(2)}, u32[]{:S(2)}) collective-permute-start(bf16[512,512]{1,0:T(8,128)(2,1)S(1)} %stack.26.refs_1_), channel_id=1, source_target_pairs={{0,4},{4,8},{8,12},{12,0},{1,5},{5,9},{9,13},{13,1},{2,6},{6,10},{... | collective-permute-start | bytes 1572872 | tf_op jit(solution)/shard_map/ppermute | solution.py:411
  121.3 14.6 %collective-permute-start.42 = (bf16[512,512]{1,0:T(8,128)(2,1)S(1)}, bf16[512,512]{1,0:T(8,128)(2,1)S(1)}, u32[]{:S(2)}, u32[]{:S(2)}) collective-permute-start(bf16[512,512]{1,0:T(8,128)(2,1)S(1)} %stack.27.refs_3_), channel_id=1, source_target_pairs={{0,1},{1,0},{2,3},{3,2},{4,5},{5,4},{6,7},{7,6},{8,9},{9,8},{10,11... | collective-permute-start | bytes 1572872 | tf_op jit(solution)/shard_map/ppermute | solution.py:411
  121.4 14.5 %collective-permute-start.41 = (bf16[512,512]{1,0:T(8,128)(2,1)S(1)}, bf16[512,512]{1,0:T(8,128)(2,1)S(1)}, u32[]{:S(2)}, u32[]{:S(2)}) collective-permute-start(bf16[512,512]{1,0:T(8,128)(2,1)S(1)} %stack.26.refs_1_), channel_id=1, source_target_pairs={{0,1},{1,0},{2,3},{3,2},{4,5},{5,4},{6,7},{7,6},{8,9},{9,8},{10,11... | collective-permute-start | bytes 1572872 | tf_op jit(solution)/shard_map/ppermute | solution.py:411
  121.9 14.6 %collective-permute-start.31 = (bf16[512,512]{1,0:T(8,128)(2,1)S(1)}, bf16[512,512]{1,0:T(8,128)(2,1)S(1)}, u32[]{:S(2)}, u32[]{:S(2)}) collective-permute-start(bf16[512,512]{1,0:T(8,128)(2,1)S(1)} %stack.26.refs_1_), channel_id=1, source_target_pairs={{0,12},{4,0},{8,4},{12,8},{1,13},{5,1},{9,5},{13,9},{2,14},{6,2},{... | collective-permute-start | bytes 1572872 | tf_op jit(solution)/shard_map/ppermute | solution.py:411
  131.8 8.3 %collective-permute-start.29 = (bf16[256,512]{1,0:T(8,128)(2,1)S(1)}, bf16[256,512]{1,0:T(8,128)(2,1)S(1)}, u32[]{:S(2)}, u32[]{:S(2)}) collective-permute-start(bf16[256,512]{1,0:T(8,128)(2,1)S(1)} %slice.17), channel_id=1, source_target_pairs={{0,16},{16,32},{32,48},{48,0},{1,17},{17,33},{33,49},{49,1},{2,18}... | collective-permute-start | bytes 786440 | tf_op jit(solution)/shard_map/ppermute | solution.py:411
  135.9 13.0 %collective-permute-start.38 = (bf16[512,512]{1,0:T(8,128)(2,1)S(1)}, bf16[512,512]{1,0:T(8,128)(2,1)S(1)}, u32[]{:S(2)}, u32[]{:S(2)}) collective-permute-start(bf16[512,512]{1,0:T(8,128)(2,1)S(1)} %collective-permute-done.28.refs_3_), channel_id=1, source_target_pairs={{0,1},{1,0},{2,3},{3,2},{4,5},{5,4},{6,7},{7,6},{8,9},{9,8},{10,11... | collective-permute-start | bytes 1572872 | tf_op jit(solution)/shard_map/ppermute | solution.py:411
  136.5 13.0 %collective-permute-start.40 = (bf16[512,512]{1,0:T(8,128)(2,1)S(1)}, bf16[512,512]{1,0:T(8,128)(2,1)S(1)}, u32[]{:S(2)}, u32[]{:S(2)}) collective-permute-start(bf16[512,512]{1,0:T(8,128)(2,1)S(1)} %collective-permute-done.34.refs_7_), channel_id=1, source_target_pairs={{0,1},{1,0},{2,3},{3,2},{4,5},{5,4},{6,7},{7,6},{8,9},{9,8},{10,11... | collective-permute-start | bytes 1572872 | tf_op jit(solution)/shard_map/ppermute | solution.py:411
  140.1 9.4 %collective-permute-start.37 = (bf16[512,512]{1,0:T(8,128)(2,1)S(1)}, bf16[512,512]{1,0:T(8,128)(2,1)S(1)}, u32[]{:S(2)}, u32[]{:S(2)}) collective-permute-start(bf16[512,512]{1,0:T(8,128)(2,1)S(1)} %collective-permute-done.13.refs_1_), channel_id=1, source_target_pairs={{0,1},{1,0},{2,3},{3,2},{4,5},{5,4},{6,7},{7,6},{8,9},{9,8},{10,11... | collective-permute-start | bytes 1572872 | tf_op jit(solution)/shard_map/ppermute | solution.py:411
  140.1 8.8 %collective-permute-start.32 = (bf16[256,512]{1,0:T(8,128)(2,1)S(1)}, bf16[256,512]{1,0:T(8,128)(2,1)S(1)}, u32[]{:S(2)}, u32[]{:S(2)}) collective-permute-start(bf16[256,512]{1,0:T(8,128)(2,1)S(1)} %slice.18), channel_id=1, source_target_pairs={{0,12},{4,0},{8,4},{12,8},{1,13},{5,1},{9,5},{13,9},{2,14},{6,2},{... | collective-permute-start | bytes 786440 | tf_op jit(solution)/shard_map/ppermute | solution.py:411
  143.5 10.4 %collective-permute-start.39 = (bf16[512,512]{1,0:T(8,128)(2,1)S(1)}, bf16[512,512]{1,0:T(8,128)(2,1)S(1)}, u32[]{:S(2)}, u32[]{:S(2)}) collective-permute-start(bf16[512,512]{1,0:T(8,128)(2,1)S(1)} %collective-permute-done.31.refs_5_), channel_id=1, source_target_pairs={{0,1},{1,0},{2,3},{3,2},{4,5},{5,4},{6,7},{7,6},{8,9},{9,8},{10,11... | collective-permute-start | bytes 1572872 | tf_op jit(solution)/shard_map/ppermute | solution.py:411
  (21 other events, 196.2 us)
